TPU v7x, 256 devices: a whole 4x4x8 slice. The times are simulated.
256 devices in a mesh: blk: 32 (over x, y, z_lo), uly: 8 (over z_hi, core).
Axes of the slice: x: 4, y: 4, z: 8 (z_hi: 4, z_lo: 2; z = z_hi * 2 + z_lo), core: 2. Of those that a mesh axis runs over, the one named last changes fastest.
Arguments:
- self_query: bfloat16 [10240, 5120], P(('blk', 'uly')), may hold values from -8 to 8
- self_key: bfloat16 [10240, 5120], P(('blk', 'uly')), may hold values from -8 to 8
- self_value: bfloat16 [10240, 5120], P(('blk', 'uly')), may hold values from -6 to 6
- cross_query: bfloat16 [10240, 5120], P(('blk', 'uly')), may hold values from -8 to 8
- text_key: bfloat16 [512, 5120], P('blk', 'uly'), may hold values from -8 to 8
- text_value: bfloat16 [512, 5120], P('blk', 'uly'), may hold values from -6 to 6
- padded_count: int32 [1], replicated, may hold values from 0 to 2560
Outputs:
- self_out: bfloat16 [10240, 5120], P(('blk', 'uly'))
- cross_out: bfloat16 [10240, 5120], P(('blk', 'uly'))
All inputs are finite; a program needn't handle non-finite values.
Results may differ from a plain program's by a relative error of at most 0.0099.
Values may be sent and summed in bfloat16 or wider, within the bound.
A program may use at most 128 MiB of HBM per device.

v0:
```python
import math

import jax
import jax.numpy as jnp
from jax import lax
from jax.sharding import Mesh
from jax.sharding import PartitionSpec as P

HD = 128
TH = 4
TW = 10
ROW_TILES = 8
BLK = ("blk_0", "blk_1", "blk_2")
ULY = ("uly_0", "uly_1")
BLK_ULY = ("blk_0", "blk_1", "blk_2", "uly_0", "uly_1")


neg_fill = -1e30


def in_blocks(x, dim, devices):
    shape = x.shape
    blocks = x.reshape(*shape[:dim], devices, shape[dim] // devices, *shape[dim + 1 :])
    return jnp.moveaxis(blocks, dim, 0)


def joined_along(blocks, dim):
    blocks = jnp.moveaxis(blocks, 0, dim)
    shape = blocks.shape
    return blocks.reshape(*shape[:dim], shape[dim] * shape[dim + 1], *shape[dim + 2 :])


def exchange_in_order(blocks, axes, order):
    inside = blocks.shape[1:]
    whole = blocks.reshape(*(lax.axis_size(a) for a in axes), *inside)
    for k in order:
        whole = lax.all_to_all(whole, axes[k], k, k, tiled=True)
    return whole.reshape(-1, *inside)


def core_and_chips(x, groups, order, split_dim, concat_dim):
    devices = lax.axis_size(groups[0]) * lax.axis_size(groups[1])
    blocks = in_blocks(x, split_dim, devices)
    return joined_along(exchange_in_order(blocks, groups, order), concat_dim)


def side_by_side(arrays, axis, dim, along):
    ends, at = ([], 0)
    for a in arrays[:-1]:
        at += a.shape[along]
        ends.append(at)
    both = jnp.concatenate(arrays, axis=along)
    return tuple(jnp.split(lax.all_gather(both, axis, axis=dim, tiled=True), ends, axis=along))


def all_blocks(x, axes, order):
    blocks = x[None]
    for k in order:
        blocks = lax.all_gather(blocks, axes[k], axis=0, tiled=True)
    held = [lax.axis_size(axes[k]) for k in reversed(order)]
    blocks = blocks.reshape(*held, *x.shape)
    turned = sorted(range(len(order)), key=lambda place: order[len(order) - 1 - place])
    return blocks.transpose(*turned, *range(len(order), blocks.ndim)).reshape(-1, *x.shape)


def gathered_by_axis(x, axes, order, dim):
    return joined_along(all_blocks(x, axes, order), dim)


def rope_tables(raster, head_size, grid_height, grid_width):
    frame_cells = grid_height * grid_width
    frame_index = raster // frame_cells
    row_index = raster // grid_width % grid_height
    col_index = raster % grid_width
    pair_index = lax.iota(jnp.int32, head_size) // 2
    side_pairs = head_size // 6
    first_pairs = head_size // 2 - 2 * side_pairs
    in_frames = pair_index < first_pairs
    in_rows = pair_index < first_pairs + side_pairs
    numerator = jnp.where(
        in_frames,
        pair_index,
        jnp.where(in_rows, pair_index - first_pairs, pair_index - first_pairs - side_pairs),
    ).astype(jnp.float32)
    denominator = jnp.where(in_frames, first_pairs, side_pairs).astype(jnp.float32)
    omegas = jnp.power(jnp.float32(10000.0), -(numerator / denominator))
    position = jnp.where(
        in_frames[None, :],
        frame_index[:, None],
        jnp.where(in_rows[None, :], row_index[:, None], col_index[:, None]),
    ).astype(jnp.float32)
    angles = position * omegas[None, :]
    return (jnp.cos(angles), jnp.sin(angles))


def rotate(values, cosine_table, sine_table):
    channels = values.shape[1]
    repeats = channels // cosine_table.shape[1]
    widened = values.astype(jnp.float32)
    channel = lax.iota(jnp.int32, channels)
    partner = jnp.where(
        channel % 2 == 0, -jnp.roll(widened, -1, axis=1), jnp.roll(widened, 1, axis=1)
    )
    return (
        widened * jnp.tile(cosine_table, (1, repeats))
        + partner * jnp.tile(sine_table, (1, repeats))
    ).astype(jnp.bfloat16)


def block_size(row_count):
    if row_count <= 2048:
        return row_count
    return 2048


def attend_step(current, queries, key_heads, value_heads, key_mask, scaling):
    maxima, totals, accumulated = current
    scores = (
        jnp.einsum("qhd,hkd->qhk", queries, key_heads, preferred_element_type=jnp.float32) * scaling
    )
    if key_mask is not None:
        scores = jnp.where(key_mask[None, None, :], scores, neg_fill)
    new_peak = jnp.maximum(maxima, jnp.max(scores, axis=2))
    weights = jnp.exp(scores - new_peak[:, :, None])
    shrink = jnp.exp(maxima - new_peak)
    totals = totals * shrink + jnp.sum(weights, axis=2)
    accumulated = accumulated * shrink[:, :, None] + jnp.einsum(
        "qhk,hkd->qhd",
        weights.astype(jnp.bfloat16),
        value_heads,
        preferred_element_type=jnp.float32,
    )
    return (new_peak, totals, accumulated)


def attend_rows(current, queries, key_heads, value_heads, key_mask, scaling):
    head_count = key_heads.shape[0]
    row_count = key_heads.shape[1]
    head_size = key_heads.shape[2]
    step_rows = block_size(row_count)
    if step_rows == row_count:
        return attend_step(current, queries, key_heads, value_heads, key_mask, scaling)
    block_count = row_count // step_rows
    key_blocks = key_heads.reshape(head_count, block_count, step_rows, head_size).transpose(
        1, 0, 2, 3
    )
    value_blocks = value_heads.reshape(head_count, block_count, step_rows, head_size).transpose(
        1, 0, 2, 3
    )
    mask_blocks = key_mask.reshape(block_count, step_rows)

    def advance_masked(carried, blocks):
        return (attend_step(carried, queries, blocks[0], blocks[1], blocks[2], scaling), None)

    current, unused = lax.scan(advance_masked, current, (key_blocks, value_blocks, mask_blocks))
    return current


def finish(current):
    maxima, totals, accumulated = current
    return (accumulated / totals[:, :, None]).reshape(accumulated.shape[0], -1).astype(jnp.bfloat16)


def head_major(rows, head_count, head_size):
    return rows.reshape(rows.shape[0], head_count, head_size).transpose(1, 0, 2)


def body(self_query, self_key, self_value, cross_query, text_key, text_value, padded_count):
    blocks_count = lax.axis_size(BLK)
    groups_count = lax.axis_size(ULY)
    tile_height = TH
    tile_width = TW
    head_size = HD
    channels = self_query.shape[1]
    group_width = channels // groups_count
    head_count = group_width // head_size
    grid_height = tile_height * ROW_TILES
    grid_width = tile_width * groups_count
    shard_rows = tile_height * grid_width
    token_total = blocks_count * shard_rows
    valid_count = token_total - padded_count[0]
    scaling = 1.0 / math.sqrt(head_size)
    block_index = lax.axis_index(BLK)
    local_index = lax.iota(jnp.int32, shard_rows)
    shaped_query = self_query.reshape(tile_height, 1, tile_width, channels)
    shaped_key = self_key.reshape(tile_height, 1, tile_width, channels)
    shaped_value = self_value.reshape(tile_height, 1, tile_width, channels)
    shaped_cross = cross_query.reshape(tile_height, 1, tile_width, channels)
    exchanged = (
        core_and_chips(shaped_query, ("uly_0", "uly_1"), (1, 0), 3, 1),
        core_and_chips(shaped_key, ("uly_0", "uly_1"), (1, 0), 3, 1),
        core_and_chips(shaped_value, ("uly_0", "uly_1"), (1, 0), 3, 1),
        core_and_chips(shaped_cross, ("uly_0", "uly_1"), (1, 0), 3, 1),
    )
    own_raster = block_index * shard_rows + local_index
    cosine_table, sine_table = rope_tables(own_raster, head_size, grid_height, grid_width)
    queries = rotate(
        exchanged[0].reshape(shard_rows, group_width), cosine_table, sine_table
    ).reshape(shard_rows, head_count, head_size)
    keys_local = head_major(
        rotate(exchanged[1].reshape(shard_rows, group_width), cosine_table, sine_table),
        head_count,
        head_size,
    )
    values_local = head_major(exchanged[2].reshape(shard_rows, group_width), head_count, head_size)
    cross_rows = exchanged[3].reshape(shard_rows, head_count, head_size)
    text_keys_heads = head_major(text_key, head_count, head_size)
    text_values_heads = head_major(text_value, head_count, head_size)

    def empty_state():
        return (
            jnp.full((shard_rows, head_count), neg_fill, jnp.float32),
            jnp.zeros((shard_rows, head_count), jnp.float32),
            jnp.zeros((shard_rows, head_count, head_size), jnp.float32),
        )

    pieces = side_by_side((keys_local, values_local), BLK, 1, 0)
    key_mask = lax.iota(jnp.int32, pieces[0].shape[1]) < valid_count
    self_state = attend_rows(empty_state(), queries, pieces[0], pieces[1], key_mask, scaling)
    text_rows = (
        gathered_by_axis(text_keys_heads, BLK, (2, 0, 1), 1),
        gathered_by_axis(text_values_heads, BLK, (2, 0, 1), 1),
    )
    cross_state = attend_rows(empty_state(), cross_rows, text_rows[0], text_rows[1], None, scaling)
    self_result = finish(self_state)
    cross_result = finish(cross_state)
    token_rows = self_query.shape[0]
    self_grid = self_result.reshape(groups_count, token_rows, 1, group_width)
    cross_grid = cross_result.reshape(groups_count, token_rows, 1, group_width)
    returned = (
        lax.all_to_all(self_grid, ULY, split_axis=0, concat_axis=2, tiled=True),
        lax.all_to_all(cross_grid, ULY, split_axis=0, concat_axis=2, tiled=True),
    )
    return (returned[0].reshape(token_rows, channels), returned[1].reshape(token_rows, channels))


def solution(mesh):
    split = Mesh(mesh.devices.reshape(4, 4, 2, 4, 2), ("blk_0", "blk_1", "blk_2", "uly_0", "uly_1"))
    in_specs = (
        P(BLK_ULY, None),
        P(BLK_ULY, None),
        P(BLK_ULY, None),
        P(BLK_ULY, None),
        P(BLK, ULY),
        P(BLK, ULY),
        P(),
    )
    out_specs = (P(BLK_ULY, None), P(BLK_ULY, None))
    return jax.shard_map(body, mesh=split, in_specs=in_specs, out_specs=out_specs, check_vma=False)
```

profile of v0, /device:TPU:1, one launch (start us, length us, event | category | flops | bytes accessed | tf_op | source)
XLA Modules:
  0.0 841.8 jit_solution(2417281264248505206)
XLA Ops:
  7.2 1.1 copy.133
  8.5 0.9 copy.92
  9.4 6.7 all-to-all-start
  17.5 3.6 all-to-all-start.4
  21.2 0.9 copy.93
  22.4 4.0 all_to_all.70
  26.5 6.5 all-to-all-start.1
  34.8 1.6 fusion.49
  36.4 7.8 all-to-all-done.1
  44.2 4.3 all-to-all-start.5
  49.7 1.4 fusion.66
  51.1 7.3 all-to-all-done.5
  58.5 4.1 all-to-all-start.3
  62.7 1.1 copy.151
  63.9 1.3 reshape.395
  65.2 3.0 maximum_negate_fusion
  68.1 1.5 copy.95
  69.6 1.6 copy.97
  71.2 1.5 copy.96
  72.6 1.6 copy.98
  74.6 1.2 maximum_negate_fusion.1
  75.8 1.5 copy.109
  77.3 1.6 copy.111
  78.9 1.3 copy.110
  80.2 2.8 copy.112
  82.9 1.1 copy.154
  84.0 1.3 reshape_reshape_reshape.3
  85.4 4.0 add_convert_fusion
  89.9 1.1 copy.103
  91.4 8.7 %all_to_all.71 = bf16[4,2,4,1,10,640]{5,2,4,3,0,1:T(4,128)(2,1)S(1)} all-to-all(bf16[4,2,4,1,10,640]{5,2,4,3,0,1:T(4,128)(2,1)S(1)} %copy.122), channel_id=1, replica_groups=mesh['blk_0'=4,'blk_1'=4,'blk_2'=2,'uly_0'=4,'uly_1'=2] {'uly_1'}, dimensions={1} | all-to-all | bytes 819200 | tf_op jit(solution)/shard_map/all_to_all | solution.py:37
  101.0 6.8 all-to-all-start.8
  107.9 15.9 %all-gather = bf16[10,16,128]{2,1,0:T(8,128)(2,1)S(1)} all-gather(bf16[5,16,128]{2,1,0:T(8,128)(2,1)S(1)} %copy.118), channel_id=2, replica_groups=mesh['blk_0'=4,'blk_1'=4,'blk_2'=2,'uly_0'=4,'uly_1'=2] {'blk_2'}, dimensions={0}, use_global_device_ids=true | all-gather | bytes 61440 | tf_op jit(solution)/shard_map/all_gather | solution.py:59
  123.8 10.7 %all_gather.23 = bf16[8,5,16,128]{3,2,1,0:T(8,128)(2,1)S(1)} all-gather(bf16[2,5,16,128]{3,2,1,0:T(8,128)(2,1)S(1)} %bitcast.224), channel_id=1, replica_groups=mesh['blk_0'=4,'blk_1'=4,'blk_2'=2,'uly_0'=4,'uly_1'=2] {'blk_0'}, dimensions={0}, use_global_device_ids=true | all-gather | bytes 204800 | tf_op jit(solution)/shard_map/all_gather | solution.py:59
  134.5 14.6 %all_gather.24 = bf16[32,5,16,128]{3,2,1,0:T(8,128)(2,1)S(1)} all-gather(bf16[8,5,16,128]{3,2,1,0:T(8,128)(2,1)S(1)} %all_gather.23), channel_id=1, replica_groups=mesh['blk_0'=4,'blk_1'=4,'blk_2'=2,'uly_0'=4,'uly_1'=2] {'blk_1'}, dimensions={0}, use_global_device_ids=true | all-gather | bytes 819200 | tf_op jit(solution)/shard_map/all_gather | solution.py:59
  150.0 4.3 all-gather.1
  154.3 11.7 %all_gather.26 = bf16[8,5,16,128]{3,2,1,0:T(8,128)(2,1)S(1)} all-gather(bf16[2,5,16,128]{3,2,1,0:T(8,128)(2,1)S(1)} %bitcast.225), channel_id=1, replica_groups=mesh['blk_0'=4,'blk_1'=4,'blk_2'=2,'uly_0'=4,'uly_1'=2] {'blk_0'}, dimensions={0}, use_global_device_ids=true | all-gather | bytes 204800 | tf_op jit(solution)/shard_map/all_gather | solution.py:59
  166.0 14.3 %all_gather.27 = bf16[32,5,16,128]{3,2,1,0:T(8,128)(2,1)S(1)} all-gather(bf16[8,5,16,128]{3,2,1,0:T(8,128)(2,1)S(1)} %all_gather.26), channel_id=1, replica_groups=mesh['blk_0'=4,'blk_1'=4,'blk_2'=2,'uly_0'=4,'uly_1'=2] {'blk_1'}, dimensions={0}, use_global_device_ids=true | all-gather | bytes 819200 | tf_op jit(solution)/shard_map/all_gather | solution.py:59
  181.8 1.0 fusion.27
  182.9 1.4 fusion.42
  184.6 1.2 convert_element_type.125
  185.9 19.9 %all-to-all-start.9 = ((bf16[8,40,1,640]{3,1,2,0:T(8,128)(2,1)}), bf16[8,40,1,640]{3,1,2,0:T(8,128)(2,1)S(1)}, u32[]{:S(2)}, u32[]{:S(2)}) async-start(bf16[8,40,1,640]{3,1,2,0:T(8,128)(2,1)} %bitcast.46), calls=%async_computation.9 | async-start | bytes 819200 | tf_op jit(solution)/shard_map/all_to_all | solution.py:232
  205.8 471.1 %all-gather.4.cloned.1.call-done = bf16[10,10240,128]{2,1,0:T(8,128)(2,1)} async-done(((bf16[10,320,128]{2,1,0:T(8,128)(2,1)}), bf16[10,10240,128]{2,1,0:T(8,128)(2,1)}) %all-gather.4.cloned.1.call-update) | async-done | bytes 26214416 | tf_op jit(solution)/shard_map/all_gather | solution.py:53
  676.9 13.7 %fusion.62 = (bf16[5,10240,128]{2,1,0:T(8,128)(2,1)}, bf16[5,10240,128]{2,1,0:T(8,128)(2,1)S(1)}) fusion(bf16[10,10240,128]{2,1,0:T(8,128)(2,1)} %all-gather.4.cloned.1.call-done), kind=kLoop, calls=%fused_computation.90 | loop fusion | bytes 52428800 | tf_op jit(solution)/shard_map/split | solution.py:53
  690.6 5.4 copy.150
  695.9 114.9 %while.15 = (s32[]{:T(128)}, f32[320,5]{0,1:T(8,128)S(1)}, f32[320,5]{0,1:T(8,128)S(1)}, f32[320,5,128]{2,0,1:T(8,128)}, pred[5,2048]{1,0:T(8,128)(4,1)S(1)}, /*...) while((s32[]{:T(128)}, f32[320,5]{0,1:T(8,128)S(1)}, ...), condition=%wide.region_3.4_spmd.clone, body=%wide.region_0.3_spmd.clone.sunk | while | flops 1714388736 | bytes 99155088 | solution.py:155
  696.0 8.5 %bitcast_reduce_fusion.3 = (f32[320,5]{0,1:T(8,128)S(1)}, f32[5,2048,320]{1,2,0:T(8,128)}) fusion(pred[2048]{0:T(1024)(128)(4,1)S(1)} %dynamic-slice_reduce_fusion.2, bf16[320,5,128]{2,0,1:T(8,128)(2,1)S(1)} %get-tuple-element.235, bf16[5,5,2048,128]{3,2,1,0:T(8,128)(2,1)} %get-tuple-element.234, s32[]{:T(128)} %get-tuple-element.219), kind=kOutput, calls=%fused_computation.1.clone.1 | convolution fusion | flops 848689600 | bytes 16147200 | tf_op jit(solution)/shard_map/while/body/eval_jaxpr/qhd,hkd->qhk/dot_general | solution.py:119
  704.5 7.6 fusion.79
  712.9 5.9 fusion.81
  718.8 8.5 %bitcast_reduce_fusion.3 = (f32[320,5]{0,1:T(8,128)S(1)}, f32[5,2048,320]{1,2,0:T(8,128)}) fusion(pred[2048]{0:T(1024)(128)(4,1)S(1)} %dynamic-slice_reduce_fusion.2, bf16[320,5,128]{2,0,1:T(8,128)(2,1)S(1)} %get-tuple-element.235, bf16[5,5,2048,128]{3,2,1,0:T(8,128)(2,1)} %get-tuple-element.234, s32[]{:T(128)} %get-tuple-element.219), kind=kOutput, calls=%fused_computation.1.clone.1 | convolution fusion | flops 848689600 | bytes 16147200 | tf_op jit(solution)/shard_map/while/body/eval_jaxpr/qhd,hkd->qhk/dot_general | solution.py:119
  727.3 7.6 fusion.79
  735.8 6.0 fusion.81
  741.9 8.5 %bitcast_reduce_fusion.3 = (f32[320,5]{0,1:T(8,128)S(1)}, f32[5,2048,320]{1,2,0:T(8,128)}) fusion(pred[2048]{0:T(1024)(128)(4,1)S(1)} %dynamic-slice_reduce_fusion.2, bf16[320,5,128]{2,0,1:T(8,128)(2,1)S(1)} %get-tuple-element.235, bf16[5,5,2048,128]{3,2,1,0:T(8,128)(2,1)} %get-tuple-element.234, s32[]{:T(128)} %get-tuple-element.219), kind=kOutput, calls=%fused_computation.1.clone.1 | convolution fusion | flops 848689600 | bytes 16147200 | tf_op jit(solution)/shard_map/while/body/eval_jaxpr/qhd,hkd->qhk/dot_general | solution.py:119
  750.3 7.6 fusion.79
  758.8 6.0 fusion.81
  764.9 8.5 %bitcast_reduce_fusion.3 = (f32[320,5]{0,1:T(8,128)S(1)}, f32[5,2048,320]{1,2,0:T(8,128)}) fusion(pred[2048]{0:T(1024)(128)(4,1)S(1)} %dynamic-slice_reduce_fusion.2, bf16[320,5,128]{2,0,1:T(8,128)(2,1)S(1)} %get-tuple-element.235, bf16[5,5,2048,128]{3,2,1,0:T(8,128)(2,1)} %get-tuple-element.234, s32[]{:T(128)} %get-tuple-element.219), kind=kOutput, calls=%fused_computation.1.clone.1 | convolution fusion | flops 848689600 | bytes 16147200 | tf_op jit(solution)/shard_map/while/body/eval_jaxpr/qhd,hkd->qhk/dot_general | solution.py:119
  773.3 7.6 fusion.79
  781.8 6.0 fusion.81
  787.9 8.5 %bitcast_reduce_fusion.3 = (f32[320,5]{0,1:T(8,128)S(1)}, f32[5,2048,320]{1,2,0:T(8,128)}) fusion(pred[2048]{0:T(1024)(128)(4,1)S(1)} %dynamic-slice_reduce_fusion.2, bf16[320,5,128]{2,0,1:T(8,128)(2,1)S(1)} %get-tuple-element.235, bf16[5,5,2048,128]{3,2,1,0:T(8,128)(2,1)} %get-tuple-element.234, s32[]{:T(128)} %get-tuple-element.219), kind=kOutput, calls=%fused_computation.1.clone.1 | convolution fusion | flops 848689600 | bytes 16147200 | tf_op jit(solution)/shard_map/while/body/eval_jaxpr/qhd,hkd->qhk/dot_general | solution.py:119
  796.4 7.6 fusion.79
  804.8 6.0 fusion.81
  810.8 1.4 divide_convert_fusion
  812.6 1.2 convert_element_type.122
  813.8 6.8 all-to-all-start.6
  821.4 12.8 %all-to-all-done.6 = bf16[8,40,1,640]{3,1,2,0:T(8,128)(2,1)S(1)} async-done(((bf16[8,40,1,640]{3,1,2,0:T(8,128)(2,1)}), bf16[8,40,1,640]{3,1,2,0:T(8,128)(2,1)S(1)}, u32[]{:S(2)}, u32[]{:S(2)}) %all-to-all-start.6) | async-done | bytes 409632 | tf_op jit(solution)/shard_map/all_to_all | solution.py:231
  (103 shorter events, 15.9 us)
Async XLA Ops:
  7.2 8.9 %copy-start.5 = (bf16[40,5120]{1,0:T(8,128)(2,1)S(1)}, bf16[40,5120]{1,0:T(8,128)(2,1)}, u32[]{:S(2)}) copy-start(bf16[40,5120]{1,0:T(8,128)(2,1)} %param.9) | copy-start | bytes 1228804
  7.2 10.0 %copy-start.6 = (bf16[40,5120]{1,0:T(8,128)(2,1)S(1)}, bf16[40,5120]{1,0:T(8,128)(2,1)}, u32[]{:S(2)}) copy-start(bf16[40,5120]{1,0:T(8,128)(2,1)} %param.11) | copy-start | bytes 1228804
  9.4 8.1 all-to-all-start
  17.5 4.9 all-to-all-start.4
  26.5 17.8 %all-to-all-start.1 = ((bf16[4,2,4,1,10,640]{5,2,4,3,1,0:T(4,128)(2,1)}), bf16[4,2,4,1,10,640]{5,2,4,3,1,0:T(4,128)(2,1)S(1)}, u32[]{:S(2)}, u32[]{:S(2)}) async-start(bf16[4,2,4,1,10,640]{5,2,4,3,1,0:T(4,128)(2,1)} %copy.93), calls=%async_computation.1 | async-start | bytes 819200 | tf_op jit(solution)/shard_map/all_to_all | solution.py:37
  44.2 14.2 %all-to-all-start.5 = ((bf16[4,2,4,1,10,640]{5,2,4,3,1,0:T(4,128)(2,1)}), bf16[4,2,4,1,10,640]{5,2,4,3,1,0:T(4,128)(2,1)}, u32[]{:S(2)}, u32[]{:S(2)}) async-start(bf16[4,2,4,1,10,640]{5,2,4,3,1,0:T(4,128)(2,1)} %copy.107), calls=%async_computation.5 | async-start | bytes 819200 | tf_op jit(solution)/shard_map/all_to_all | solution.py:37
  58.5 24.5 %all-to-all-start.3 = ((bf16[4,2,4,1,10,640]{5,2,4,3,1,0:T(4,128)(2,1)}), bf16[4,2,4,1,10,640]{5,2,4,3,1,0:T(4,128)(2,1)}, u32[]{:S(2)}, u32[]{:S(2)}) async-start(bf16[4,2,4,1,10,640]{5,2,4,3,1,0:T(4,128)(2,1)} %copy.101), calls=%async_computation.3 | async-start | bytes 819200 | tf_op jit(solution)/shard_map/all_to_all | solution.py:37
  62.6 614.3 %all-gather.4.cloned.1.call-start = ((), (), s32[]{:S(2)}) async-start(), calls=%async_computation.10 | async-start | bytes 27033600 | tf_op jit(solution)/shard_map/all_gather | solution.py:53
  78.9 6.5 copy-start.1
  80.2 5.2 copy-start.4
  85.4 4.0 copy-start.3
  89.4 1.6 copy-start.7
  91.0 16.9 %copy-start.8 = (bf16[16,640]{1,0:T(8,128)(2,1)S(1)}, bf16[16,640]{1,0:T(8,128)(2,1)}, u32[]{:S(2)}) copy-start(bf16[16,640]{1,0:T(8,128)(2,1)} %param.13) | copy-start | bytes 61444
  91.4 58.6 %copy-start.9 = (bf16[16,640]{1,0:T(8,128)(2,1)S(1)}, bf16[16,640]{1,0:T(8,128)(2,1)}, u32[]{:S(2)}) copy-start(bf16[16,640]{1,0:T(8,128)(2,1)} %param.14) | copy-start | bytes 61444
  101.0 79.5 %all-to-all-start.8 = ((bf16[4,2,4,1,10,640]{5,2,4,3,1,0:T(4,128)(2,1)}), bf16[4,2,4,1,10,640]{5,2,4,3,1,0:T(4,128)(2,1)S(1)}, u32[]{:S(2)}, u32[]{:S(2)}) async-start(bf16[4,2,4,1,10,640]{5,2,4,3,1,0:T(4,128)(2,1)} %copy.123), calls=%async_computation.8 | async-start | bytes 819200 | tf_op jit(solution)/shard_map/all_to_all | solution.py:37
  149.0 31.4 %copy-start.2 = (bf16[320,5,128]{2,1,0:T(8,128)(2,1)S(1)}, bf16[320,5,128]{2,1,0:T(8,128)(2,1)}, u32[]{:S(2)}) copy-start(bf16[320,5,128]{2,1,0:T(8,128)(2,1)} %get-tuple-element.136) | copy-start | bytes 1228804
  185.9 628.0 %all-to-all-start.9 = ((bf16[8,40,1,640]{3,1,2,0:T(8,128)(2,1)}), bf16[8,40,1,640]{3,1,2,0:T(8,128)(2,1)S(1)}, u32[]{:S(2)}, u32[]{:S(2)}) async-start(bf16[8,40,1,640]{3,1,2,0:T(8,128)(2,1)} %bitcast.46), calls=%async_computation.9 | async-start | bytes 819200 | tf_op jit(solution)/shard_map/all_to_all | solution.py:232
  704.5 8.5 %copy-start = (f32[5,2048,320]{1,2,0:T(8,128)S(1)}, f32[5,2048,320]{1,2,0:T(8,128)}, u32[]{:S(2)}) copy-start(f32[5,2048,320]{1,2,0:T(8,128)} %get-tuple-element.206) | copy-start | bytes 39321604 | tf_op jit(solution)/shard_map/while
  727.3 8.5 %copy-start = (f32[5,2048,320]{1,2,0:T(8,128)S(1)}, f32[5,2048,320]{1,2,0:T(8,128)}, u32[]{:S(2)}) copy-start(f32[5,2048,320]{1,2,0:T(8,128)} %get-tuple-element.206) | copy-start | bytes 39321604 | tf_op jit(solution)/shard_map/while
  750.3 8.5 %copy-start = (f32[5,2048,320]{1,2,0:T(8,128)S(1)}, f32[5,2048,320]{1,2,0:T(8,128)}, u32[]{:S(2)}) copy-start(f32[5,2048,320]{1,2,0:T(8,128)} %get-tuple-element.206) | copy-start | bytes 39321604 | tf_op jit(solution)/shard_map/while
  773.3 8.5 %copy-start = (f32[5,2048,320]{1,2,0:T(8,128)S(1)}, f32[5,2048,320]{1,2,0:T(8,128)}, u32[]{:S(2)}) copy-start(f32[5,2048,320]{1,2,0:T(8,128)} %get-tuple-element.206) | copy-start | bytes 39321604 | tf_op jit(solution)/shard_map/while
  796.4 8.5 %copy-start = (f32[5,2048,320]{1,2,0:T(8,128)S(1)}, f32[5,2048,320]{1,2,0:T(8,128)}, u32[]{:S(2)}) copy-start(f32[5,2048,320]{1,2,0:T(8,128)} %get-tuple-element.206) | copy-start | bytes 39321604 | tf_op jit(solution)/shard_map/while
  813.8 20.4 %all-to-all-start.6 = ((bf16[8,40,1,640]{3,1,2,0:T(8,128)(2,1)}), bf16[8,40,1,640]{3,1,2,0:T(8,128)(2,1)S(1)}, u32[]{:S(2)}, u32[]{:S(2)}) async-start(bf16[8,40,1,640]{3,1,2,0:T(8,128)(2,1)} %bitcast.23), calls=%async_computation.6 | async-start | bytes 819200 | tf_op jit(solution)/shard_map/all_to_all | solution.py:231
Sparse Core Ops, SparseCore 0:
  91.1 585.6 all-gather.3
where the time goes:
time: 843 us; the launch traced here: 842 us
  waiting for transfers between devices  499 us (59%)
  blocking collectives  84.1 us (10%)
  matrix products  74.5 us (9%)
  local copies, waits for them, and re-layouts  59 us (7%)
  starting transfers between devices  58.8 us (7%)
  other arithmetic  50.9 us (6%)
  between operations  15.1 us (2%)
    all_gather x1, waiting for transfers between devices, side_by_side(): lax.all_gather(both, axis, axis=dim, tiled=True)  471 us
    all_gather x6, blocking collectives, all_blocks(): blocks = lax.all_gather(blocks, axes[k], axis=0, tiled=True)  71.3 us
    dot_general x6, matrix products, attend_step(): jnp.einsum('qhd,hkd->qhk', queries, key_heads, preferred_element_type=jnp...  43 us
    reduce_sum x6, other arithmetic, attend_step(): totals = totals * shrink + jnp.sum(weights, axis=2)  39 us
    all_to_all x6, starting transfers between devices, exchange_in_order(): whole = lax.all_to_all(whole, axes[k], k, k, tiled=True)  32 us
    dot_general x6, matrix products, attend_step(): jnp.einsum('qhk,hkd->qhd', weights.astype(jnp.bfloat16), value_heads, pre...  31.5 us
    all_to_all x1, starting transfers between devices, body(): lax.all_to_all(cross_grid, ULY, split_axis=0, concat_axis=2, tiled=True)  19.9 us
  transfers between devices with their start and end apart: 9, of which 5 were waited for; matrix products, arithmetic and copies ran while one was open for 20% of the time, Pallas kernels for 0%

commit v1 on v0

v1 whole, which is shorter than its diff:
```python
import functools
import math

import jax
import jax.numpy as jnp
import numpy as np
from jax import lax
from jax.experimental import pallas as pl
from jax.experimental.pallas import tpu as pltpu
from jax.sharding import Mesh
from jax.sharding import PartitionSpec as P

HD = 128
TH = 4
TW = 10
TOK = TH * TW
ROW_TILES = 8
NX, NY, NZ, NC = 4, 4, 8, 2
LAYER = 5
HEADS = NZ * LAYER
GRID_H = TH * ROW_TILES
GRID_W = TW * NZ
KEYS = NX * NY * NZ * NC * TOK
LAST = KEYS // NX
PAD = 24
GROUPS = 16
ULY = ("uly_0", "uly_1")
BLK = ("blk_0", "blk_1", "blk_2")
NEG = -1e30
MESH = pl.DeviceIdType.MESH


def place():
    x = lax.axis_index("blk_0")
    y = lax.axis_index("blk_1")
    z = lax.axis_index("uly_0") * 2 + lax.axis_index("blk_2")
    return x, y, z, lax.axis_index("uly_1")


def at_xz(x, z):
    return {"blk_0": x, "uly_0": z // 2, "blk_2": lax.rem(z, 2)}


def prep_kernel(cos_ref, sin_ref, q_ref, k_ref, v_ref, c_ref, qo, ko, vo, co):
    cos = cos_ref[...]
    sin = sin_ref[...]
    even = lax.rem(lax.broadcasted_iota(jnp.int32, (TOK, HD), 1), 2) == 0
    for h in range(LAYER):
        cut = slice(h * HD, (h + 1) * HD)
        for src, dst in ((q_ref, qo), (k_ref, ko)):
            wide = src[:, cut].astype(jnp.float32)
            swapped = jnp.where(even, pltpu.roll(wide, HD - 1, 1), pltpu.roll(wide, 1, 1))
            dst[h] = (wide * cos + swapped * sin).astype(jnp.bfloat16)
        vo[h] = v_ref[:, cut]
        co[h] = c_ref[:, cut]


def prep(cos, sin, arrays):
    table = pl.BlockSpec((TOK, HD), lambda i: (0, 0))
    wide = pl.BlockSpec((TOK, LAYER * HD), lambda i: (0, i))
    heads = pl.BlockSpec((LAYER, TOK, HD), lambda i: (i, 0, 0))
    return pl.pallas_call(
        prep_kernel,
        grid=(NZ,),
        in_specs=[table, table] + [wide] * 4,
        out_specs=[heads] * 4,
        out_shape=[jax.ShapeDtypeStruct((HEADS, TOK, HD), jnp.bfloat16)] * 4,
        name="prep",
    )(cos, sin, *arrays)


def gather_kernel(q, c, k, v, qa, ca, qb, cb, ka, va, kb, vb, send, recv, ring_send, ring_recv, twin_send, twin_recv):
    x, y, z, core = place()
    twin = {"uly_1": 1 - core}
    yp, ym, yo = lax.rem(y + 1, NY), lax.rem(y + NY - 1, NY), lax.rem(y + 2, NY)
    xp, xm, xo = lax.rem(x + 1, NX), lax.rem(x + NX - 1, NX), lax.rem(x + 2, NX)

    barrier = pltpu.get_barrier_semaphore()

    def greet(n, carry):
        peer = at_xz(lax.rem(x + n // NZ, NX), lax.rem(z + lax.rem(n, NZ), NZ))
        pl.semaphore_signal(barrier, inc=1, device_id=peer, device_id_type=MESH)
        return carry

    lax.fori_loop(1, NX * NZ, greet, 0)
    for peer in ({"blk_1": yp}, {"blk_1": ym}, twin):
        pl.semaphore_signal(barrier, inc=1, device_id=peer, device_id_type=MESH)
    pl.semaphore_wait(barrier, NX * NZ - 1 + 3)

    own_a, own_b = z * LAYER + x, z * LAYER + LAYER - 1
    pltpu.make_async_copy(q.at[own_b], qb.at[z], recv.at[0]).start()
    pltpu.make_async_copy(c.at[own_b], cb.at[z], recv.at[1]).start()
    pltpu.make_async_copy(k.at[own_b], kb.at[x, core, y, z], recv.at[2]).start()
    pltpu.make_async_copy(v.at[own_b], vb.at[x, core, y, z], recv.at[3]).start()
    pltpu.make_async_copy(q.at[own_a], qa.at[x, z], recv.at[4]).start()
    pltpu.make_async_copy(c.at[own_a], ca.at[x, z], recv.at[5]).start()
    pltpu.make_async_copy(k.at[own_a], ka.at[x, core, y, z], recv.at[6]).start()
    pltpu.make_async_copy(v.at[own_a], va.at[x, core, y, z], recv.at[7]).start()

    def push(src, dst, s, r, peer):
        pltpu.make_async_remote_copy(src, dst, send.at[s], recv.at[r], device_id=peer, device_id_type=MESH).start()

    def send_b(n, carry):
        tz = lax.rem(z + n, NZ)
        h, peer = tz * LAYER + LAYER - 1, at_xz(x, tz)
        push(k.at[h], kb.at[x, core, y, z], 2, 2, peer)
        push(v.at[h], vb.at[x, core, y, z], 3, 3, peer)
        return carry

    def send_a(n, carry):
        tx, tz = lax.rem(x + n // NZ, NX), lax.rem(z + lax.rem(n, NZ), NZ)
        h, peer = tz * LAYER + tx, at_xz(tx, tz)
        push(k.at[h], ka.at[x, core, y, z], 2, 6, peer)
        push(v.at[h], va.at[x, core, y, z], 3, 7, peer)
        return carry

    def send_qb(n, carry):
        tz = lax.rem(z + n, NZ)
        h, peer = tz * LAYER + LAYER - 1, at_xz(x, tz)
        push(q.at[h], qb.at[z], 0, 0, peer)
        push(c.at[h], cb.at[z], 1, 1, peer)
        return carry

    def send_qa(n, carry):
        tx, tz = lax.rem(x + n // NZ, NX), lax.rem(z + lax.rem(n, NZ), NZ)
        h, peer = tz * LAYER + tx, at_xz(tx, tz)
        push(q.at[h], qa.at[x, z], 0, 4, peer)
        push(c.at[h], ca.at[x, z], 1, 5, peer)
        return carry

    lax.fori_loop(1, NZ, send_b, 0)
    lax.fori_loop(1, NX * NZ, send_a, 0)
    lax.fori_loop(1, NZ, send_qb, 0)
    lax.fori_loop(1, NX * NZ, send_qa, 0)

    def arrived(ref, sem):
        pltpu.make_async_copy(ref, ref, sem).wait()

    def give(kind, region, axis, target, slot):
        for t, arr in enumerate(kind):
            pltpu.make_async_remote_copy(
                region(arr), region(arr), ring_send.at[slot, t], ring_recv.at[slot, t],
                device_id={axis: target}, device_id_type=MESH).start()

    def took(kind, region, slot):
        for t, arr in enumerate(kind):
            arrived(region(arr), ring_recv.at[slot, t])

    def share(kind, region, slot):
        for t, arr in enumerate(kind):
            pltpu.make_async_remote_copy(
                region(arr), region(arr), twin_send.at[slot, t], twin_recv.at[slot, t],
                device_id=twin, device_id_type=MESH).start()

    b, a = (kb, vb), (ka, va)
    b_y = lambda yy: lambda r: r.at[x, core, yy]
    b_half = lambda yy, s: lambda r: r.at[x, core, yy, pl.ds(4 * s, 4)]
    a_y = lambda yy: lambda r: r.at[:, core, yy]
    a_half = lambda yy, s: lambda r: r.at[pl.ds(2 * s, 2), core, yy]
    b_x = lambda xx: lambda r: r.at[xx, core]
    bx_half = lambda xx, s: lambda r: r.at[xx, core, pl.ds(2 * s, 2)]

    for t in range(2):
        arrived(b_y(y)(b[t]), recv.at[2 + t])
    give(b, b_y(y), "blk_1", yp, 0)
    give(b, b_y(y), "blk_1", ym, 1)
    for t in range(2):
        arrived(a_y(y)(a[t]), recv.at[6 + t])
    give(a, a_y(y), "blk_1", yp, 4)
    give(a, a_y(y), "blk_1", ym, 5)
    share(a, a_y(y), 0)
    took(b, b_y(ym), 0)
    give(b, b_half(ym, 0), "blk_1", yp, 2)
    took(b, b_y(yp), 1)
    give(b, b_half(yp, 1), "blk_1", ym, 3)
    took(b, b_half(yo, 0), 2)
    took(b, b_half(yo, 1), 3)
    give(b, b_x(x), "blk_0", xp, 8)
    give(b, b_x(x), "blk_0", xm, 9)
    share(b, b_x(x), 4)
    took(a, a_y(ym), 4)
    give(a, a_half(ym, 0), "blk_1", yp, 6)
    share(a, a_y(ym), 1)
    took(a, a_y(yp), 5)
    give(a, a_half(yp, 1), "blk_1", ym, 7)
    share(a, a_y(yp), 2)
    took(b, b_x(xm), 8)
    give(b, bx_half(xm, 0), "blk_0", xp, 10)
    share(b, b_x(xm), 5)
    took(b, b_x(xp), 9)
    give(b, bx_half(xp, 1), "blk_0", xm, 11)
    share(b, b_x(xp), 6)
    took(a, a_half(yo, 0), 6)
    took(a, a_half(yo, 1), 7)
    share(a, a_y(yo), 3)
    took(b, bx_half(xo, 0), 10)
    took(b, bx_half(xo, 1), 11)
    share(b, b_x(xo), 7)

    arrived(qb, recv.at[0])
    arrived(cb, recv.at[1])
    arrived(qa, recv.at[4])
    arrived(ca, recv.at[5])
    other = 1 - core
    for slot in range(4):
        for t in range(2):
            yy = (y, ym, yp, yo)[slot]
            arrived(a[t].at[:, other, yy], twin_recv.at[slot, t])
            xx = (x, xm, xp, xo)[slot]
            arrived(b[t].at[xx, other], twin_recv.at[4 + slot, t])
    for s, ref in enumerate((q, c, k, v)):
        arrived(ref.at[pl.ds(0, NX * NZ - 1 + NZ - 1)], send.at[s])
    for t in range(2):
        for slot in (0, 1):
            arrived(b_y(y)(b[t]), ring_send.at[slot, t])
            arrived(a_y(y)(a[t]), ring_send.at[4 + slot, t])
            arrived(b_x(x)(b[t]), ring_send.at[8 + slot, t])
            arrived(b_half(y, slot)(b[t]), ring_send.at[2 + slot, t])
            arrived(a_half(y, slot)(a[t]), ring_send.at[6 + slot, t])
            arrived(bx_half(x, slot)(b[t]), ring_send.at[10 + slot, t])
        for slot in range(4):
            arrived(a_y(y)(a[t]), twin_send.at[slot, t])
            arrived(b_x(x)(b[t]), twin_send.at[4 + slot, t])


def gather(q, c, k, v):
    any_spec = pl.BlockSpec(memory_space=pl.ANY)
    shapes = [(NX, NZ)] * 2 + [(NZ,)] * 2 + [(NX, NC, NY, NZ)] * 4
    dma = pltpu.SemaphoreType.DMA
    return pl.pallas_call(
        gather_kernel,
        in_specs=[any_spec] * 4,
        out_specs=[any_spec] * 8,
        out_shape=[jax.ShapeDtypeStruct((*s, TOK, HD), jnp.bfloat16) for s in shapes],
        scratch_shapes=[dma((4,)), dma((8,)), dma((12, 2)), dma((12, 2)), dma((8, 2)), dma((8, 2))],
        compiler_params=pltpu.CompilerParams(collective_id=0, has_side_effects=True),
        name="gather",
    )(q, c, k, v)


def attend_kernel(scaling, block, blocks, masked, rows, *refs):
    if masked:
        q_ref, k_ref, v_ref, perm_ref, bias_ref, o_ref, vt, s0, s1, ot = refs
    else:
        q_ref, k_ref, v_ref, perm_ref, o_ref, vt, s0, s1, ot = refs
        bias_ref = None
    step = pl.program_id(0)
    steps = pl.num_programs(0)
    scale = scaling * math.log2(math.e)
    q = q_ref[...]

    @pl.when(step == 0)
    def _():
        @pl.loop(0, blocks)
        def _(j):
            cut = pl.ds(pl.multiple_of(j * block, block), block)
            vt[:, cut] = v_ref[cut, :].T

    def scores(j, into, with_bias):
        start = pl.multiple_of(j * block, block)
        s = lax.dot_general(k_ref[pl.ds(start, block), :], q, (((1,), (1,)), ((), ())),
                            preferred_element_type=jnp.float32)
        if with_bias:
            off = pl.multiple_of((j - (blocks - masked)) * block, block)
            bias = bias_ref[pl.ds(off, block), 0:1]
            s = s + bias
        into[...] = s
        return jnp.max(s, axis=0, keepdims=True)

    def absorb(j, held, peak, state):
        m, l, acc = state
        start = pl.multiple_of(j * block, block)
        new = jnp.maximum(m, peak)
        shrink = jnp.exp2((m - new) * scale)
        p = jnp.exp2((held[...] - new) * scale)
        l = l * shrink + jnp.sum(p, axis=0, keepdims=True)
        acc = acc * shrink + jnp.dot(vt[:, pl.ds(start, block)], p.astype(jnp.bfloat16),
                                     preferred_element_type=jnp.float32)
        return new, l, acc

    state = (jnp.full((1, rows), NEG, jnp.float32), jnp.zeros((1, rows), jnp.float32),
             jnp.zeros((HD, rows), jnp.float32))
    plain = blocks - masked
    first = scores(0, s0, False)

    def pair(bias_1, bias_0):
        def run(i, carry):
            peak, state = carry
            j = i * 2
            peak_1 = scores(j + 1, s1, bias_1)
            state = absorb(j, s0, peak, state)
            peak = scores(jnp.minimum(j + 2, blocks - 1), s0, bias_0)
            state = absorb(j + 1, s1, peak_1, state)
            return peak, state
        return run

    carry = (first, state)
    if masked:
        carry = lax.fori_loop(0, plain // 2 - 1, pair(False, False), carry)
        carry = lax.fori_loop(plain // 2 - 1, plain // 2, pair(False, True), carry)
        carry = lax.fori_loop(plain // 2, blocks // 2, pair(True, True), carry)
    else:
        carry = lax.fori_loop(0, blocks // 2, pair(False, False), carry)
    m, l, acc = carry[1]
    out_t = (acc / l).astype(jnp.bfloat16)
    ot[:, pl.ds(pl.multiple_of(step * rows, 128), rows)] = out_t

    @pl.when(step == steps - 1)
    def _():
        for n in range(o_ref.shape[0]):
            o_ref[n] = lax.dot_general(
                perm_ref[...], ot[:, n * NZ * TOK : (n + 1) * NZ * TOK], (((1,), (1,)), ((), ())),
                preferred_element_type=jnp.float32).astype(jnp.bfloat16)


def attend(q, k, v, perm, bias, rows, block, scaling, name):
    total, keys = q.shape[0], k.shape[0]
    blocks = keys // block
    masked = 0 if bias is None else LAST // block
    outs = total // (NZ * TOK)
    whole = lambda a: pl.BlockSpec(a.shape, lambda i: (0,) * a.ndim)
    args = [q, k, v, perm] + ([] if bias is None else [bias])
    return pl.pallas_call(
        functools.partial(attend_kernel, scaling, block, blocks, masked, rows),
        grid=(total // rows,),
        in_specs=[pl.BlockSpec((rows, HD), lambda i: (i, 0))] + [whole(a) for a in args[1:]],
        out_specs=pl.BlockSpec((outs, GROUPS * PAD, HD), lambda i: (0, 0, 0)),
        out_shape=jax.ShapeDtypeStruct((outs, GROUPS * PAD, HD), jnp.bfloat16),
        scratch_shapes=[
            pltpu.VMEM((HD, keys), jnp.bfloat16),
            pltpu.VMEM((block, rows), jnp.float32),
            pltpu.VMEM((block, rows), jnp.float32),
            pltpu.VMEM((HD, total), jnp.bfloat16),
        ],
        cost_estimate=pl.CostEstimate(flops=4 * total * keys * HD, bytes_accessed=4 * keys * HD,
                                      transcendentals=total * keys),
        name=name,
    )(*args)


def order_matrix():
    perm = np.zeros((GROUPS * PAD, NZ * TOK), np.float32)
    for zl in range(2):
        for a in range(2):
            for i in range(TH):
                for zh2 in range(2):
                    for j in range(TW):
                        row = (zl * 8 + a * 4 + i) * PAD + zh2 * TW + j
                        perm[row, (2 * (2 * a + zh2) + zl) * TOK + i * TW + j] = 1
    return jnp.asarray(perm, jnp.bfloat16)


def deliver_kernel(sa, ca, sb, cb, rs, rc, send, recv, near):
    x, y, z, core = place()
    zl, zh = lax.axis_index("blk_2"), lax.axis_index("uly_0")
    barrier = pltpu.get_barrier_semaphore()
    count = NX * NZ * NC

    def target(n):
        tx = lax.rem(x + n // (NZ * NC), NX)
        rest = lax.rem(n, NZ * NC)
        ti = lax.rem(zh + rest // 4, 4)
        tl = lax.rem(zl + lax.rem(rest // 2, 2), 2)
        ta = lax.rem(core + lax.rem(rest, 2), 2)
        return tx, ti, tl, ta, {"blk_0": tx, "uly_0": ti, "blk_2": tl, "uly_1": ta}

    def greet(n, carry):
        pl.semaphore_signal(barrier, inc=1, device_id=target(n)[-1], device_id_type=MESH)
        return carry

    lax.fori_loop(1, count, greet, 0)
    pl.semaphore_wait(barrier, count - 1)

    head_a, head_b = z * LAYER + x, z * LAYER + LAYER - 1
    own = zl * 8 + core * 4 + zh
    for n, (a, b, r) in enumerate(((sa, sb, rs), (ca, cb, rc))):
        pltpu.make_async_copy(a.at[x, own], r.at[head_a, core], near.at[n, 0]).start()
        pltpu.make_async_copy(b.at[own], r.at[head_b, core], near.at[n, 1]).start()

    def push(src, dst, n, peer):
        pltpu.make_async_remote_copy(src, dst, send.at[n], recv.at[n], device_id=peer, device_id_type=MESH).start()

    def send_b(n, carry):
        tx, ti, tl, ta, peer = target(n)
        g = tl * 8 + ta * 4 + ti
        push(sb.at[g], rs.at[head_b, core], 0, peer)
        push(cb.at[g], rc.at[head_b, core], 1, peer)
        return carry

    def send_a(n, carry):
        tx, ti, tl, ta, peer = target(n)
        g = tl * 8 + ta * 4 + ti
        push(sa.at[tx, g], rs.at[head_a, core], 0, peer)
        push(ca.at[tx, g], rc.at[head_a, core], 1, peer)
        return carry

    lax.fori_loop(1, NZ * NC, send_b, 0)
    lax.fori_loop(1, count, send_a, 0)

    def arrived(ref, sem):
        pltpu.make_async_copy(ref, ref, sem).wait()

    for n, (a, b, r) in enumerate(((sa, sb, rs), (ca, cb, rc))):
        arrived(r.at[head_a, core], near.at[n, 0])
        arrived(r.at[head_b, core], near.at[n, 1])
        moved = r.at[pl.ds(0, (count - 1 + NZ * NC - 1) // 2)]
        arrived(moved, recv.at[n])
        arrived(moved, send.at[n])


def deliver(sa, ca, sb, cb):
    any_spec = pl.BlockSpec(memory_space=pl.ANY)
    dma = pltpu.SemaphoreType.DMA
    return pl.pallas_call(
        deliver_kernel,
        in_specs=[any_spec] * 4,
        out_specs=[any_spec] * 2,
        out_shape=[jax.ShapeDtypeStruct((HEADS, NC, PAD, HD), jnp.bfloat16)] * 2,
        scratch_shapes=[dma((2,)), dma((2,)), dma((2, 2))],
        compiler_params=pltpu.CompilerParams(collective_id=1, has_side_effects=True),
        name="deliver",
    )(sa, ca, sb, cb)


def rope_tables(frame, row, col):
    pair = lax.iota(jnp.int32, HD) // 2
    side = HD // 6
    first = HD // 2 - 2 * side
    in_frames = pair < first
    in_rows = pair < first + side
    numerator = jnp.where(in_frames, pair, jnp.where(in_rows, pair - first, pair - first - side)).astype(jnp.float32)
    denominator = jnp.where(in_frames, first, side).astype(jnp.float32)
    omegas = jnp.power(jnp.float32(10000.0), -(numerator / denominator))
    position = jnp.where(in_frames[None, :], frame[:, None],
                         jnp.where(in_rows[None, :], row[:, None], col[:, None])).astype(jnp.float32)
    angles = position * omegas[None, :]
    sign = jnp.where(lax.iota(jnp.int32, HD) % 2 == 0, -1.0, 1.0)
    return jnp.cos(angles), jnp.sin(angles) * sign[None, :]


def body(self_query, self_key, self_value, cross_query, text_key, text_value, padded_count):
    scaling = 1.0 / math.sqrt(HD)
    x, y, z, core = place()
    zl, zh = lax.axis_index("blk_2"), lax.axis_index("uly_0")

    rows = text_key.shape[0]
    text = jnp.stack([text_key, text_value]).reshape(2, rows, LAYER, HD).transpose(0, 2, 1, 3)
    text = lax.ppermute(text, ("blk_2", "uly_1"), [(0, 0), (1, 2), (2, 1), (3, 3)])
    text = lax.all_gather(text, ("blk_0", "blk_1", "uly_1"), axis=2, tiled=True)

    token = lax.iota(jnp.int32, TOK)
    block = (x * NY + y) * 2 + zl
    row = lax.rem(block, ROW_TILES) * TH + token // TW
    col = (zh * 2 + core) * TW + token % TW
    cos, sin = rope_tables(jnp.full((TOK,), block // ROW_TILES), row, col)
    qh, kh, vh, ch = prep(cos, sin, (self_query, self_key, self_value, cross_query))

    qa, ca, qb, cb, ka, va, kb, vb = gather(qh, ch, kh, vh)

    order = lax.iota(jnp.int32, LAST)
    n_t, n_z, n_y, n_c = order % TOK, order // TOK % NZ, order // (TOK * NZ) % NY, order // (TOK * NZ * NY)
    n_row = (n_y * 2 + n_z % 2) * TH + n_t // TW
    n_col = (n_z // 2 * 2 + n_c) * TW + n_t % TW
    index = (NX - 1) * GRID_H * GRID_W + n_row * GRID_W + n_col
    bias = jnp.where(index < KEYS - padded_count[0], 0.0, NEG).astype(jnp.float32)
    bias = jnp.broadcast_to(bias[:, None], (LAST, HD))

    perm = order_matrix()
    flat = lambda t: t.reshape(-1, HD)
    text_a = lax.dynamic_index_in_dim(text, x, 1, keepdims=False)
    cross_a = attend(flat(ca), text_a[0], text_a[1], perm, None, 256, 256, scaling, "cross_a")
    cross_b = attend(flat(cb), text[0, LAYER - 1], text[1, LAYER - 1], perm, None, NZ * TOK, 256, scaling, "cross_b")
    self_a = attend(flat(qa), flat(ka), flat(va), perm, bias, 256, 1280, scaling, "self_a")
    self_b = attend(flat(qb), flat(kb), flat(vb), perm, bias, NZ * TOK, 1280, scaling, "self_b")

    split_a = lambda o: o.reshape(NX, GROUPS, PAD, HD)
    split_b = lambda o: o.reshape(GROUPS, PAD, HD)
    results = deliver(split_a(self_a), split_a(cross_a), split_b(self_b), split_b(cross_b))

    def finish(r):
        r = r[:, :, : 2 * TW].reshape(HEADS, NC, 2, TW, HD)
        return r.transpose(2, 1, 3, 0, 4).reshape(TOK, HEADS * HD)

    return finish(results[0]), finish(results[1])


def solution(mesh):
    split = Mesh(mesh.devices.reshape(4, 4, 2, 4, 2), BLK + ULY)
    own = P(BLK + ULY, None)
    return jax.shard_map(body, mesh=split, in_specs=(own,) * 4 + (P(BLK, ULY),) * 2 + (P(),),
                         out_specs=(own, own), check_vma=False)
```

time: 843 us -> 193 us (0.23)
  waiting for transfers between devices: 499 us -> 1.69 us
  Pallas kernels: 0 us -> 162 us
  blocking collectives: 84.1 us -> 0 us
  matrix products: 74.5 us -> 0 us
  starting transfers between devices: 58.8 us -> 4.96 us
  local copies, waits for them, and re-layouts: 59 us -> 8.63 us
  other arithmetic: 50.9 us -> 0.87 us
    all_gather x1, waiting for transfers between devices: 471 us -> 0.01 us  [body(): text = lax.all_gather(text, ('blk_0', 'blk_1', 'uly_1'), axis=2, tiled=True)]
    pallas_call x0 -> x7, Pallas kernels: none -> 162 us  [the longest x1 77.5 us: gather(): pl.pallas_call(gather_kernel, in_specs=[any_spec] * 4, out_specs=[any_spe...]
    dot_general x12 -> x0, matrix products: 74.5 us -> none  [the longest x6 43 us: attend_step(): jnp.einsum('qhd,hkd->qhk', queries, key_heads, preferred_element_type=jnp...]
    all_gather x6 -> x0, blocking collectives: 71.3 us -> none  [all_blocks(): blocks = lax.all_gather(blocks, axes[k], axis=0, tiled=True)]
    all_to_all x8 -> x0, starting transfers between devices: 58.7 us -> none  [the longest x6 32 us: exchange_in_order(): whole = lax.all_to_all(whole, axes[k], k, k, tiled=True)]
    reduce_sum x6 -> x0, other arithmetic: 39 us -> none  [attend_step(): totals = totals * shrink + jnp.sum(weights, axis=2)]
    all_to_all x8 -> x0, waiting for transfers between devices: 28.3 us -> none  [the longest x6 15.5 us: exchange_in_order(): whole = lax.all_to_all(whole, axes[k], k, k, tiled=True)]
    split x1 -> x0, local copies, waits for them, and re-layouts: 13.7 us -> none  [side_by_side(): jnp.split(lax.all_gather(both, axis, axis=dim, tiled=True), ends, axis=al...]
  transfers between devices with their start and end apart: 9 -> 2, of which waited for: 5 -> 1; matrix products, arithmetic and copies ran while one was open for 20% -> 1% of each run, Pallas kernels for 0% -> 61%
where the time goes in v1:
time: 193 us
  Pallas kernels  162 us (84%)
  between operations  14.8 us (8%)
  local copies, waits for them, and re-layouts  8.63 us (4%)
  starting transfers between devices  4.96 us (3%)
    pallas_call x1, Pallas kernels, gather(): pl.pallas_call(gather_kernel, in_specs=[any_spec] * 4, out_specs=[any_spe...  77.5 us
    pallas_call x4, Pallas kernels, attend(): pl.pallas_call(functools.partial(attend_kernel, scaling, block, blocks, m...  43.9 us
    pallas_call x1, Pallas kernels, deliver(): pl.pallas_call(deliver_kernel, in_specs=[any_spec] * 4, out_specs=[any_sp...  34.7 us
    pallas_call x1, Pallas kernels, prep(): pl.pallas_call(prep_kernel, grid=(NZ,), in_specs=[table, table] + [wide]...  5.56 us
    ppermute x1, starting transfers between devices, body(): lax.ppermute(text, ('blk_2', 'uly_1'), [(0, 0), (1, 2), (2, 1), (3, 3)])  4.92 us
  transfers between devices with their start and end apart: 2, of which 1 were waited for; matrix products, arithmetic and copies ran while one was open for 1% of the time, Pallas kernels for 61%

profile of v1, /device:TPU:1, one launch (start us, length us, event | category | flops | bytes accessed | tf_op | source)
XLA Modules:
  0.0 192.6 jit_solution(13263307833573118476)
XLA Ops:
  7.2 0.0 all-gather.2.cloned.1.call-start
  7.2 0.8 stack.9
  8.0 0.8 stack.10
  8.8 4.9 %collective-permute-start = (bf16[2,5,16,128]{3,2,1,0:T(8,128)(2,1)S(1)}, bf16[2,5,16,128]{3,2,1,0:T(8,128)(2,1)S(1)}, u32[]{:S(2)}, u32[]{:S(2)}) collective-permute-start(bf16[2,5,16,128]{3,2,1,0:T(8,128)(2,1)S(1)} %maximum_bitcast_fusion), channel_id=1, source_target_pairs={{0,0},{1,8},{8,1},{9,9},{2,2},{3,10},{10,3},{11,11},{4,4},{5,12},{... | collective-permute-start | bytes 122888 | tf_op jit(solution)/shard_map/ppermute | solution.py:448
  13.7 1.7 collective-permute-done
  15.4 0.0 copy-start.1
  15.4 0.6 copy-done.1
  16.0 0.0 all-gather.2.cloned.1.call-update
  16.8 0.8 sine_multiply_fusion
  17.5 5.6 %prep.1 = (bf16[40,40,128]{2,1,0:T(8,128)(2,1)}, bf16[40,40,128]{2,1,0:T(8,128)(2,1)}, bf16[40,40,128]{2,1,0:T(8,128)(2,1)}, bf16[40,40,128]{2,1,0:T(8,128)(2,1)}) custom-call(f32[40,128]{1,0:T(8,128)} %get-tuple-element.35.cos_ref, f32[40,128]{1,0:T(8,128)} %get-tuple-element.34.sin_ref, bf16[40,5120]{1,0:T(8,128)(2,1)} %q_ref.1, bf16[40,5120]{1,0:T(8,128)(2,1)} %k_ref.1, ...), custom_call_target="tpu_custom_call" | custom-call | tf_op jit(solution)/shard_map/prep/pallas_call | solution.py:62
  23.1 77.5 %gather.1 = (bf16[4,8,40,128]{3,2,1,0:T(8,128)(2,1)}, bf16[4,8,40,128]{3,2,1,0:T(8,128)(2,1)}, bf16[8,40,128]{2,1,0:T(8,128)(2,1)}, bf16[8,40,128]{2,1,0:T(8,128...) custom-call(bf16[40,40,128]{2,1,0:T(8,128)(2,1)} %get-tuple-element., ...), custom_call_target="tpu_custom_call" | custom-call | tf_op jit(solution)/shard_map/gather/pallas_call | solution.py:230
  100.6 0.1 compare_select_fusion
  100.7 1.5 broadcast_in_dim.81.refs_4_
  102.2 9.9 %self_b.1 = bf16[1,384,128]{2,1,0:T(8,128)(2,1)} custom-call(bf16[320,128]{1,0:T(8,128)(2,1)} %bitcast.57, bf16[10240,128]{1,0:T(8,128)(2,1)} %bitcast.41, bf16[10240,128]{1,0:T(8,128)(2,1)} %bitcast.42, bf16[384,320]{1,0:T(8,128)(2,1)} %constant.189.clone.refs_3_, f32[2560,128]{1,0:T(8,128)} %broadcast_in_dim.81.refs_4_), custom_call_target="tpu_custom_call" | custom-call | flops 1677721600 | bytes 5242880 | tf_op jit(solution)/shard_map/self_b/pallas_call | solution.py:323
  112.1 25.5 %self_a.1 = bf16[4,384,128]{2,1,0:T(8,128)(2,1)} custom-call(bf16[1280,128]{1,0:T(8,128)(2,1)} %bitcast.60, bf16[10240,128]{1,0:T(8,128)(2,1)} %bitcast.58, bf16[10240,128]{1,0:T(8,128)(2,1)} %bitcast.59, bf16[384,320]{1,0:T(8,128)(2,1)} %constant.189.clone.refs_3_, f32[2560,128]{1,0:T(8,128)} %broadcast_in_dim.81.refs_4_), custom_call_target="tpu_custom_call" | custom-call | flops 6710886400 | bytes 5242880 | tf_op jit(solution)/shard_map/self_a/pallas_call | solution.py:323
  137.6 0.0 all-gather.2.cloned.1.call-done
  137.6 1.9 %slice_bitcast_fusion = (bf16[512,128]{1,0:T(8,128)(2,1)}, bf16[512,128]{1,0:T(8,128)(2,1)}, bf16[512,128]{1,0:T(8,128)(2,1)}, bf16[512,128]{1,0:T(8,128)(2,1)}) fusion(bf16[2,5,512,128]{3,2,1,0:T(8,128)(2,1)} %all-gather.2.cloned.1.call-done, s32[]{:T(128)S(6)} %select_n.204, s32[]{:T(128)S(6)} %add.216), kind=kLoop, calls=%fused_computation.2 | loop fusion | bytes 1048584 | tf_op jit(solution)/shard_map/squeeze | solution.py:472
  139.5 5.8 %cross_a.1 = bf16[4,384,128]{2,1,0:T(8,128)(2,1)} custom-call(bf16[1280,128]{1,0:T(8,128)(2,1)} %bitcast.55, bf16[512,128]{1,0:T(8,128)(2,1)} %get-tuple-element.31.refs_1_, bf16[512,128]{1,0:T(8,128)(2,1)} %get-tuple-element.33.refs_2_, bf16[384,320]{1,0:T(8,128)(2,1)} %constant.189.clone.refs_3_), custom_call_target="tpu_custom_call" | custom-call | flops 335544320 | bytes 262144 | tf_op jit(solution)/shard_map/cross_a/pallas_call | solution.py:323
  145.3 2.7 %cross_b.1 = bf16[1,384,128]{2,1,0:T(8,128)(2,1)} custom-call(bf16[320,128]{1,0:T(8,128)(2,1)} %bitcast.56, bf16[512,128]{1,0:T(8,128)(2,1)} %get-tuple-element.32.refs_1_, bf16[512,128]{1,0:T(8,128)(2,1)} %get-tuple-element.30.refs_2_, bf16[384,320]{1,0:T(8,128)(2,1)} %constant.189.clone.refs_3_), custom_call_target="tpu_custom_call" | custom-call | flops 83886080 | bytes 262144 | tf_op jit(solution)/shard_map/cross_b/pallas_call | solution.py:323
  148.0 34.7 %deliver.1 = (bf16[40,2,24,128]{3,2,1,0:T(8,128)(2,1)}, bf16[40,2,24,128]{3,2,1,0:T(8,128)(2,1)}) custom-call(bf16[4,16,24,128]{3,2,1,0:T(8,128)(2,1)} %bitcast.52, bf16[4,16,24,128]{3,2,1,0:T(8,128)(2,1)} %bitcast.47, bf16[16,24,128]{2,1,0:T(8,128)(2,1)} %bitcast.54, bf16[16,24,128]{2,1,0:T(8,128)(2,1)} %bitcast.53), custom_call_target="tpu_custom_call" | custom-call | tf_op jit(solution)/shard_map/deliver/pallas_call | solution.py:414
  182.7 0.0 copy-start
  182.7 1.2 copy.20
  184.0 0.8 copy.26
  184.8 0.0 copy-done
  184.8 0.1 copy.18
  185.0 0.8 copy.27
  (8 shorter events, 0.1 us)
Async XLA Ops:
  7.2 130.4 %all-gather.2.cloned.1.call-start = ((), (), s32[]{:S(2)}) async-start(), calls=%async_computation | async-start | bytes 1351680 | tf_op jit(solution)/shard_map/all_gather | solution.py:449
  8.8 6.6 %collective-permute-start = (bf16[2,5,16,128]{3,2,1,0:T(8,128)(2,1)S(1)}, bf16[2,5,16,128]{3,2,1,0:T(8,128)(2,1)S(1)}, u32[]{:S(2)}, u32[]{:S(2)}) collective-permute-start(bf16[2,5,16,128]{3,2,1,0:T(8,128)(2,1)S(1)} %maximum_bitcast_fusion), channel_id=1, source_target_pairs={{0,0},{1,8},{8,1},{9,9},{2,2},{3,10},{10,3},{11,11},{4,4},{5,12},{... | collective-permute-start | bytes 122888 | tf_op jit(solution)/shard_map/ppermute | solution.py:448
  15.4 0.6 copy-start.1
  182.7 2.1 %copy-start = (bf16[40,2,24,128]{3,2,1,0:T(8,128)(2,1)S(1)}, bf16[40,2,24,128]{3,2,1,0:T(8,128)(2,1)}, u32[]{:S(2)}) copy-start(bf16[40,2,24,128]{3,2,1,0:T(8,128)(2,1)} %get-tuple-element.28) | copy-start | bytes 1474564
Sparse Core Ops, SparseCore 0:
  16.2 54.7 all-gather.1

commit v2 on v1

v2 whole, which is shorter than its diff:
```python
import functools
import math

import jax
import jax.numpy as jnp
import numpy as np
from jax import lax
from jax.experimental import pallas as pl
from jax.experimental.pallas import tpu as pltpu
from jax.sharding import Mesh
from jax.sharding import PartitionSpec as P

HD = 128
TH = 4
TW = 10
TOK = TH * TW
ROW_TILES = 8
NX, NY, NZ, NC = 4, 4, 8, 2
LAYER = 5
HEADS = NZ * LAYER
GRID_H = TH * ROW_TILES
GRID_W = TW * NZ
KEYS = NX * NY * NZ * NC * TOK
LAST = KEYS // NX
PAD = 24
GROUPS = 16
ULY = ("uly_0", "uly_1")
BLK = ("blk_0", "blk_1", "blk_2")
NEG = -1e30
MESH = pl.DeviceIdType.MESH


def place():
    x = lax.axis_index("blk_0")
    y = lax.axis_index("blk_1")
    z = lax.axis_index("uly_0") * 2 + lax.axis_index("blk_2")
    return x, y, z, lax.axis_index("uly_1")


def at_xz(x, z):
    return {"blk_0": x, "uly_0": z // 2, "blk_2": lax.rem(z, 2)}


def prep_kernel(cos_ref, sin_ref, q_ref, k_ref, v_ref, c_ref, qo, ko, vo, co):
    cos = cos_ref[...]
    sin = sin_ref[...]
    even = lax.rem(lax.broadcasted_iota(jnp.int32, (TOK, HD), 1), 2) == 0
    for h in range(LAYER):
        cut = slice(h * HD, (h + 1) * HD)
        for src, dst in ((q_ref, qo), (k_ref, ko)):
            wide = src[:, cut].astype(jnp.float32)
            swapped = jnp.where(even, pltpu.roll(wide, HD - 1, 1), pltpu.roll(wide, 1, 1))
            dst[h] = (wide * cos + swapped * sin).astype(jnp.bfloat16)
        vo[h] = v_ref[:, cut]
        co[h] = c_ref[:, cut]


def prep(cos, sin, arrays):
    table = pl.BlockSpec((TOK, HD), lambda i: (0, 0))
    wide = pl.BlockSpec((TOK, LAYER * HD), lambda i: (0, i))
    heads = pl.BlockSpec((LAYER, TOK, HD), lambda i: (i, 0, 0))
    return pl.pallas_call(
        prep_kernel,
        grid=(NZ,),
        in_specs=[table, table] + [wide] * 4,
        out_specs=[heads] * 4,
        out_shape=[jax.ShapeDtypeStruct((HEADS, TOK, HD), jnp.bfloat16)] * 4,
        name="prep",
    )(cos, sin, *arrays)


SPAN = NZ * TOK
REGION = NX * SPAN
WIDE = 384
TILE = 256
SCALE = math.log2(math.e) / math.sqrt(HD)
NT = (((1,), (1,)), ((), ()))


def block_kernel(
    q, c, k, v, text, bias_a, bias_b, perm,
    rs, rc, qa_h, ca_h, qb_h, cb_h, ka_h, va_h, kb_h, vb_h,
    qa, qb, ca, cb, ka, va, kb, vb, txt, s0, s1, vt, acc, row_m, row_l, ot, oa, ob, oc, od, part, stat,
    send, recv, local, ring_send, ring_recv, twin_send, twin_recv, fan_send, fan_recv, part_send, part_recv,
    text_send, text_recv, out_send, out_recv, near,
):
    x, y, z, core = place()
    zl, zh = lax.axis_index("blk_2"), lax.axis_index("uly_0")
    twin = {"uly_1": 1 - core}
    yp, ym, yo = lax.rem(y + 1, NY), lax.rem(y + NY - 1, NY), lax.rem(y + 2, NY)
    others = NX * NZ * NC - 1

    def owner(n, m):
        ti = lax.rem(zh + m // 4, 4)
        tl = lax.rem(zl + lax.rem(m // 2, 2), 2)
        ta = lax.rem(core + lax.rem(m, 2), 2)
        peer = {"blk_0": lax.rem(x + n, NX), "uly_0": ti, "blk_2": tl, "uly_1": ta}
        return tl * 8 + ta * 4 + ti, peer

    barrier = pltpu.get_barrier_semaphore()

    def greet(n, carry):
        peer = owner(n // GROUPS, lax.rem(n, GROUPS))[1]
        pl.semaphore_signal(barrier, inc=1, device_id=peer, device_id_type=MESH)
        return carry

    lax.fori_loop(1, others + 1, greet, 0)
    for yy in (yp, ym, yo):
        pl.semaphore_signal(barrier, inc=1, device_id={"blk_1": yy}, device_id_type=MESH)
    pl.semaphore_wait(barrier, others + 3)

    def arrived(ref, sem):
        pltpu.make_async_copy(ref, ref, sem).wait()

    def push(src, dst, s, r, peer):
        pltpu.make_async_remote_copy(src, dst, s, r, device_id=peer, device_id_type=MESH).start()

    own_a, own_b = z * LAYER + x, z * LAYER + LAYER - 1

    def rows(ref, start):
        return ref.at[pl.ds(pl.multiple_of(start, 8), TOK)]

    def rows_of(n):
        return n * SPAN + z * TOK

    def send_b(pairs):
        def run(n, carry):
            tz = lax.rem(z + n, NZ)
            h, peer = tz * LAYER + LAYER - 1, at_xz(x, tz)
            for s, src, r, dst in pairs:
                push(src.at[h], rows(dst, z * TOK), send.at[s], recv.at[r], peer)
            return carry
        for s, src, r, dst in pairs:
            pltpu.make_async_copy(src.at[own_b], rows(dst, z * TOK), recv.at[r]).start()
        lax.fori_loop(1, NZ, run, 0)

    def send_a(pairs, relative):
        def where(tx):
            return rows_of(lax.rem(x - tx + NX, NX)) if relative else rows_of(x)
        def run(n, carry):
            tx, tz = lax.rem(x + n // NZ, NX), lax.rem(z + lax.rem(n, NZ), NZ)
            h, peer = tz * LAYER + tx, at_xz(tx, tz)
            for s, src, r, dst in pairs:
                push(src.at[h], rows(dst, where(tx)), send.at[s], recv.at[r], peer)
            return carry
        for s, src, r, dst in pairs:
            pltpu.make_async_copy(src.at[own_a], rows(dst, where(x)), recv.at[r]).start()
        lax.fori_loop(1, NX * NZ, run, 0)

    send_b(((2, k, 0, kb_h), (3, v, 1, vb_h), (0, q, 2, qb_h)))
    for n in range(1, NX):
        tx = lax.rem(x + n, NX)
        for ab, h in ((0, tx), (1, LAYER - 1)):
            push(text.at[h], txt.at[core, y, x, ab], text_send.at[0], text_recv.at[0], {"blk_0": tx})
    for ab, h in ((0, x), (1, LAYER - 1)):
        pltpu.make_async_copy(text.at[h], txt.at[core, y, x, ab], local.at[8 + ab]).start()
    send_a(((2, k, 3, ka_h), (3, v, 4, va_h)), False)
    send_a(((0, q, 5, qa_h),), True)
    send_b(((1, c, 6, cb_h),))
    send_a(((1, c, 7, ca_h),), True)

    qb[:, SPAN:, :] = jnp.zeros((NX, WIDE - SPAN, HD), jnp.bfloat16)
    cb[SPAN:, :] = jnp.zeros((WIDE - SPAN, HD), jnp.bfloat16)
    row_m[...] = jnp.full_like(row_m, NEG)
    row_l[...] = jnp.zeros_like(row_l)
    acc[...] = jnp.zeros_like(acc)
    stat[...] = jnp.zeros_like(stat)

    def give(kind, region, target, n):
        for t, arr in enumerate(kind):
            push(region(arr), region(arr), ring_send.at[n, t], ring_recv.at[n, t], {"blk_1": target})

    def took(kind, region, n):
        for t, arr in enumerate(kind):
            arrived(region(arr), ring_recv.at[n, t])

    def share(kind, region, n):
        for t, arr in enumerate(kind):
            push(region(arr), region(arr), twin_send.at[n, t], twin_recv.at[n, t], twin)

    def land(src, dst, r, n):
        arrived(src, recv.at[r])
        pltpu.make_async_copy(src, dst, local.at[n]).start()
        return lambda: pltpu.make_async_copy(src, dst, local.at[n]).wait()

    a, b = (ka, va), (kb, vb)
    mine = core * NY
    a_y = lambda yy: lambda r: r.at[mine + yy]
    a_half = lambda yy, s: lambda r: r.at[mine + yy, pl.ds(s * (REGION // 2), REGION // 2)]
    b_y = lambda yy: lambda r: r.at[core, yy]
    b_half = lambda yy, s: lambda r: r.at[core, yy, pl.ds(s * (SPAN // 2), SPAN // 2)]
    b_all = lambda r: r.at[core]

    for done in [land(kb_h, kb.at[core, y], 0, 0), land(vb_h, vb.at[core, y], 1, 1)]:
        done()
    give(b, b_y(y), yp, 0)
    give(b, b_y(y), ym, 1)
    land(qb_h, qb.at[0, pl.ds(0, SPAN)], 2, 2)()
    for n in range(1, NX):
        push(qb.at[0, pl.ds(0, SPAN)], qb.at[NX - n, pl.ds(0, SPAN)], fan_send.at[n - 1], fan_recv.at[NX - n - 1],
             {"blk_0": lax.rem(x + n, NX)})
    arrived(txt.at[core, y, pl.ds(0, NX - 1)], text_recv.at[0])
    for ab in range(2):
        arrived(txt.at[core, y, x, ab], local.at[8 + ab])
    for yy in (yp, ym, yo):
        push(txt.at[core, y], txt.at[core, y], text_send.at[1], text_recv.at[1], {"blk_1": yy})
    took(b, b_y(ym), 0)
    give(b, b_half(ym, 0), yp, 2)
    took(b, b_y(yp), 1)
    give(b, b_half(yp, 1), ym, 3)
    took(b, b_half(yo, 0), 2)
    took(b, b_half(yo, 1), 3)
    share(b, b_all, 4)
    arrived(txt.at[core, pl.ds(0, NY - 1)], text_recv.at[1])
    push(txt.at[core], txt.at[core], text_send.at[2], text_recv.at[2], twin)
    for n in range(1, NX):
        arrived(qb.at[n, pl.ds(0, SPAN)], fan_recv.at[n - 1])

    held = (s0, s1)

    def absorb(cols, width, s, peak):
        m = row_m[0:1, cols]
        new = jnp.maximum(m, peak)
        shrink = jnp.exp2((m - new) * SCALE)
        p = jnp.exp2((s[:, :width] - new) * SCALE)
        row_m[0:1, cols] = new
        row_l[0:1, cols] = row_l[0:1, cols] * shrink + jnp.sum(p, axis=0, keepdims=True)
        acc[:, cols] = acc[:, cols] * shrink + jnp.dot(
            vt[...], p.astype(jnp.bfloat16), preferred_element_type=jnp.float32)

    def attend(queries, width, scores):
        peaks = scores(queries[0][0], s0)
        for n, (_, cols) in enumerate(queries):
            ahead = scores(queries[n + 1][0], held[(n + 1) % 2]) if n + 1 < len(queries) else None
            absorb(cols, width, held[n % 2], peaks)
            peaks = ahead

    def over(bias, width):
        return jnp.concatenate([bias] * (width // HD), axis=1)

    b_tiles = [(n, slice(n * WIDE, (n + 1) * WIDE)) for n in range(NX)]

    def b_region(i, carry):
        cc = lax.rem(core + i, NC)

        @pl.when(i == 1)
        def _():
            for t in range(2):
                arrived(b[t].at[1 - core], twin_recv.at[4, t])

        vt[...] = vb[cc].reshape(REGION, HD).T

        def scores(n, into):
            s = lax.dot_general(kb[cc].reshape(REGION, HD), qb[n], NT, preferred_element_type=jnp.float32)
            s = s + over(bias_b[pl.ds(pl.multiple_of(cc * REGION, 8), REGION), :], WIDE)
            into[...] = s
            return jnp.max(s, axis=0, keepdims=True)

        attend(b_tiles, WIDE, scores)
        return carry

    lax.fori_loop(0, NC, b_region, 0)
    for n in range(NX):
        cols = slice(n * WIDE, (n + 1) * WIDE)
        part[n] = (acc[:, cols] / row_l[0:1, cols]).astype(jnp.bfloat16)
        stat[n, 0:1, :] = row_m[0:1, cols]
        stat[n, 1:2, :] = row_l[0:1, cols]
    for n in range(1, NX):
        peer = {"blk_0": lax.rem(x + n, NX)}
        push(part.at[n], part.at[NX + n], part_send.at[n - 1, 0], part_recv.at[n - 1, 0], peer)
        push(stat.at[n], stat.at[NX + n], part_send.at[n - 1, 1], part_recv.at[n - 1, 1], peer)

    row_m[...] = jnp.full_like(row_m, NEG)
    row_l[...] = jnp.zeros_like(row_l)
    acc[...] = jnp.zeros_like(acc)

    for done in [land(ka_h, ka.at[mine + y], 3, 3), land(va_h, va.at[mine + y], 4, 4)]:
        done()
    give(a, a_y(y), yp, 4)
    give(a, a_y(y), ym, 5)
    share(a, a_y(y), 0)

    def ordered(cols):
        return lax.dot_general(perm[...], cols, NT, preferred_element_type=jnp.float32).reshape(
            GROUPS, PAD, HD).astype(jnp.bfloat16)

    def deliver(src, result, n, head, which):
        def run(m, carry):
            g, peer = owner(n, m)
            push(src.at[g], result.at[head, core], out_send.at[which], out_recv.at[which], peer)
            return carry
        lax.fori_loop(1 if n == 0 else 0, GROUPS, run, 0)

    def keep(src, result, head, n):
        return pltpu.make_async_copy(src.at[zl * 8 + core * 4 + zh], result.at[head, core], near.at[n])

    for n in range(1, NX):
        arrived(part.at[NX + n], part_recv.at[n - 1, 0])
        arrived(stat.at[NX + n], part_recv.at[n - 1, 1])
    slots = [0] + [NX + n for n in range(1, NX)]
    top = stat[0, 0:1, :]
    for n in slots[1:]:
        top = jnp.maximum(top, stat[n, 0:1, :])
    weights = [stat[n, 1:2, :] * jnp.exp2((stat[n, 0:1, :] - top) * SCALE) for n in slots]
    total = weights[0] + weights[1] + weights[2] + weights[3]
    merged = part[0].astype(jnp.float32) * (weights[0] / total)
    for n, w in zip(slots[1:], weights[1:]):
        merged = merged + part[n].astype(jnp.float32) * (w / total)
    ob[...] = ordered(merged.astype(jnp.bfloat16)[:, :SPAN])
    keep(ob, rs, own_b, 0).start()
    deliver(ob, rs, 0, own_b, 0)

    land(qa_h, qa, 5, 5)()
    a_tiles = [(slice(n * TILE, (n + 1) * TILE),) * 2 for n in range(REGION // TILE)]

    def text_rows(ab, kv):
        return txt[:, :, :, ab, kv].reshape(-1, HD)

    def cross(q_tile, keys, values_t):
        s = lax.dot_general(keys, q_tile, NT, preferred_element_type=jnp.float32)
        p = jnp.exp2((s - jnp.max(s, axis=0, keepdims=True)) * SCALE)
        weighted = jnp.dot(values_t, p.astype(jnp.bfloat16), preferred_element_type=jnp.float32)
        return (weighted / jnp.sum(p, axis=0, keepdims=True)).astype(jnp.bfloat16)

    def a_region(i, carry):
        theirs = jnp.logical_or(i == 1, jnp.logical_or(jnp.logical_or(i == 4, i == 5), i == 7))
        cc = jnp.where(theirs, 1 - core, core)
        yy = jnp.where(i < 2, y, jnp.where(i >= 6, yo, jnp.where(lax.rem(i, 2) == 0, ym, yp)))
        n = jnp.where(i < 2, 0, jnp.where(i >= 6, 3, 1 + lax.rem(i, 2)))
        at = cc * NY + yy

        @pl.when(i == 2)
        def _():
            took(a, a_y(ym), 4)
            give(a, a_half(ym, 0), yp, 6)
            share(a, a_y(ym), 1)
            took(a, a_y(yp), 5)
            give(a, a_half(yp, 1), ym, 7)
            share(a, a_y(yp), 2)

        @pl.when(i == 4)
        def _():
            took(a, a_half(yo, 0), 6)
            took(a, a_half(yo, 1), 7)
            share(a, a_y(yo), 3)
            arrived(txt.at[1 - core], text_recv.at[2])
            land(cb_h, cb.at[pl.ds(0, SPAN)], 6, 6)()
            land(ca_h, ca, 7, 7)()
            keys, values_t = text_rows(1, 0), text_rows(1, 1).T
            od[...] = ordered(cross(cb[...], keys, values_t)[:, :SPAN])
            keys, values_t = text_rows(0, 0), text_rows(0, 1).T
            for cols, _ in a_tiles:
                ot[:, cols] = cross(ca[cols, :], keys, values_t)
            for n in range(NX):
                oc[n] = ordered(ot[:, n * SPAN : (n + 1) * SPAN])
            keep(od, rc, own_b, 1).start()
            keep(oc.at[0], rc, own_a, 2).start()
            deliver(od, rc, 0, own_b, 1)
            for n in range(NX):
                deliver(oc.at[n], rc, n, own_a, 1)

        @pl.when(theirs)
        def _():
            for t in range(2):
                arrived(a[t].at[at], twin_recv.at[n, t])

        vt[...] = va[at].T

        def scores(cols, into):
            q_tile = qa[cols, :]
            s = lax.dot_general(ka[at, : REGION - SPAN, :], q_tile, NT, preferred_element_type=jnp.float32)
            into[: REGION - SPAN, :TILE] = s
            e = lax.dot_general(ka[at, REGION - SPAN :, :], q_tile, NT, preferred_element_type=jnp.float32)
            e = e + over(bias_a[pl.ds(pl.multiple_of(at * SPAN, 8), SPAN), :], TILE)
            into[REGION - SPAN :, :TILE] = e
            return jnp.maximum(jnp.max(s, axis=0, keepdims=True), jnp.max(e, axis=0, keepdims=True))

        attend(a_tiles, TILE, scores)
        return carry

    lax.fori_loop(0, NC * NY, a_region, 0)
    for cols, _ in a_tiles:
        ot[:, cols] = (acc[:, cols] / row_l[0:1, cols]).astype(jnp.bfloat16)
    for n in range(NX):
        oa[n] = ordered(ot[:, n * SPAN : (n + 1) * SPAN])
        if n == 0:
            keep(oa.at[0], rs, own_a, 3).start()
        deliver(oa.at[n], rs, n, own_a, 0)

    for s, ref in enumerate((q, c, k, v)):
        arrived(ref.at[pl.ds(0, NX * NZ - 1 + NZ - 1)], send.at[s])
    for t in range(2):
        for n in (0, 1):
            arrived(b_y(y)(b[t]), ring_send.at[n, t])
            arrived(b_half(y, 0)(b[t]), ring_send.at[2 + n, t])
            arrived(a_y(y)(a[t]), ring_send.at[4 + n, t])
            arrived(a_half(y, 0)(a[t]), ring_send.at[6 + n, t])
        for n in range(4):
            arrived(a_y(y)(a[t]), twin_send.at[n, t])
        arrived(b[t].at[core], twin_send.at[4, t])
    for n in range(1, NX):
        arrived(qb.at[n, pl.ds(0, SPAN)], fan_send.at[n - 1])
        arrived(part.at[n], part_send.at[n - 1, 0])
        arrived(stat.at[n], part_send.at[n - 1, 1])
    arrived(txt.at[core, y, pl.ds(0, NX - 1)], text_send.at[0])
    arrived(txt.at[core, pl.ds(0, NY - 1)], text_send.at[1])
    arrived(txt.at[core], text_send.at[2])
    keep(ob, rs, own_b, 0).wait()
    keep(od, rc, own_b, 1).wait()
    keep(oc.at[0], rc, own_a, 2).wait()
    keep(oa.at[0], rs, own_a, 3).wait()
    for n, r in enumerate((rs, rc)):
        moved = r.at[pl.ds(0, (others + NZ * NC - 1) // 2)]
        arrived(moved, out_recv.at[n])
        arrived(moved, out_send.at[n])


def block(q, c, k, v, text, bias_a, bias_b, perm):
    any_spec = pl.BlockSpec(memory_space=pl.ANY)
    vmem = pl.BlockSpec(memory_space=pltpu.VMEM)
    dma = pltpu.SemaphoreType.DMA
    half = lambda *s: pltpu.VMEM(s, jnp.bfloat16)
    full = lambda *s: pltpu.VMEM(s, jnp.float32)
    landing = [REGION, REGION, SPAN, SPAN, REGION, REGION, SPAN, SPAN]
    result = jax.ShapeDtypeStruct((HEADS, NC, PAD, HD), jnp.bfloat16)
    return pl.pallas_call(
        block_kernel,
        in_specs=[any_spec] * 5 + [vmem] * 3,
        out_specs=[any_spec] * 10,
        out_shape=[result] * 2 + [jax.ShapeDtypeStruct((n, HD), jnp.bfloat16) for n in landing],
        scratch_shapes=[
            half(REGION, HD), half(NX, WIDE, HD), half(REGION, HD), half(WIDE, HD),
            half(NC * NY, REGION, HD), half(NC * NY, REGION, HD), half(NC, NY, SPAN, HD), half(NC, NY, SPAN, HD),
            half(NC, NY, NX, 2, 2, 16, HD),
            full(REGION, WIDE), full(REGION, WIDE), half(HD, REGION), full(HD, NX * WIDE),
            full(8, NX * WIDE), full(8, NX * WIDE), half(HD, REGION),
            half(NX, GROUPS, PAD, HD), half(GROUPS, PAD, HD), half(NX, GROUPS, PAD, HD), half(GROUPS, PAD, HD),
            half(2 * NX, HD, WIDE), full(2 * NX, 8, WIDE),
            dma((4,)), dma((8,)), dma((10,)), dma((8, 2)), dma((8, 2)), dma((5, 2)), dma((5, 2)), dma((3,)), dma((3,)),
            dma((3, 2)), dma((3, 2)), dma((3,)), dma((3,)), dma((2,)), dma((2,)), dma((4,)),
        ],
        compiler_params=pltpu.CompilerParams(collective_id=0, has_side_effects=True),
        name="block",
    )(q, c, k, v, text, bias_a, bias_b, perm)[:2]


def order_matrix():
    perm = np.zeros((GROUPS * PAD, NZ * TOK), np.float32)
    for zl in range(2):
        for a in range(2):
            for i in range(TH):
                for zh2 in range(2):
                    for j in range(TW):
                        row = (zl * 8 + a * 4 + i) * PAD + zh2 * TW + j
                        perm[row, (2 * (2 * a + zh2) + zl) * TOK + i * TW + j] = 1
    return jnp.asarray(perm, jnp.bfloat16)


def rope_tables(frame, row, col):
    pair = lax.iota(jnp.int32, HD) // 2
    side = HD // 6
    first = HD // 2 - 2 * side
    in_frames = pair < first
    in_rows = pair < first + side
    numerator = jnp.where(in_frames, pair, jnp.where(in_rows, pair - first, pair - first - side)).astype(jnp.float32)
    denominator = jnp.where(in_frames, first, side).astype(jnp.float32)
    omegas = jnp.power(jnp.float32(10000.0), -(numerator / denominator))
    position = jnp.where(in_frames[None, :], frame[:, None],
                         jnp.where(in_rows[None, :], row[:, None], col[:, None])).astype(jnp.float32)
    angles = position * omegas[None, :]
    sign = jnp.where(lax.iota(jnp.int32, HD) % 2 == 0, -1.0, 1.0)
    return jnp.cos(angles), jnp.sin(angles) * sign[None, :]


def body(self_query, self_key, self_value, cross_query, text_key, text_value, padded_count):
    x, y, z, core = place()
    zl, zh = lax.axis_index("blk_2"), lax.axis_index("uly_0")

    rows = text_key.shape[0]
    text = jnp.stack([text_key, text_value]).reshape(2, rows, LAYER, HD).transpose(2, 0, 1, 3)
    text = lax.ppermute(text, ("blk_2", "uly_1"), [(0, 0), (1, 2), (2, 1), (3, 3)])

    token = lax.iota(jnp.int32, TOK)
    chunk = (x * NY + y) * 2 + zl
    row = lax.rem(chunk, ROW_TILES) * TH + token // TW
    col = (zh * 2 + core) * TW + token % TW
    cos, sin = rope_tables(jnp.full((TOK,), chunk // ROW_TILES), row, col)
    qh, kh, vh, ch = prep(cos, sin, (self_query, self_key, self_value, cross_query))

    order = lax.iota(jnp.int32, LAST)
    n_t, n_z, n_y, n_c = order % TOK, order // TOK % NZ, order // (TOK * NZ) % NY, order // (TOK * NZ * NY)
    n_row = (n_y * 2 + n_z % 2) * TH + n_t // TW
    n_col = (n_z // 2 * 2 + n_c) * TW + n_t % TW
    index = (NX - 1) * GRID_H * GRID_W + n_row * GRID_W + n_col
    bias = jnp.where(index < KEYS - padded_count[0], 0.0, NEG).astype(jnp.float32)
    bias_a = jnp.broadcast_to(bias[:, None], (LAST, HD))
    bias_b = jnp.broadcast_to(jnp.where(x == NX - 1, bias, 0.0)[:, None], (LAST, HD))

    results = block(qh, ch, kh, vh, text, bias_a, bias_b, order_matrix())

    def finish(r):
        r = r[:, :, : 2 * TW].reshape(HEADS, NC, 2, TW, HD)
        return r.transpose(2, 1, 3, 0, 4).reshape(TOK, HEADS * HD)

    return finish(results[0]), finish(results[1])


def solution(mesh):
    split = Mesh(mesh.devices.reshape(4, 4, 2, 4, 2), BLK + ULY)
    own = P(BLK + ULY, None)
    return jax.shard_map(body, mesh=split, in_specs=(own,) * 4 + (P(BLK, ULY),) * 2 + (P(),),
                         out_specs=(own, own), check_vma=False)
```

time: 193 us -> 112 us (0.58)
  Pallas kernels: 162 us -> 96.1 us
  between operations: 14.8 us -> 1.44 us
    pallas_call x6 -> x1, Pallas kernels: 156 us -> 90.5 us  [block(): pl.pallas_call(block_kernel, in_specs=[any_spec] * 5 + [vmem] * 3, out_sp...]
  transfers between devices with their start and end apart: 2 -> 1, of which waited for: 1 -> 0; matrix products, arithmetic and copies ran while one was open for 1% -> 1% of each run, Pallas kernels for 61% -> 5%
where the time goes in v2:
time: 112 us; the launch traced here: 111 us
  Pallas kernels  96.1 us (86%)
  local copies, waits for them, and re-layouts  7.49 us (7%)
  starting transfers between devices  4.92 us (4%)
  between operations  1.44 us (1%)
    pallas_call x1, Pallas kernels, block(): pl.pallas_call(block_kernel, in_specs=[any_spec] * 5 + [vmem] * 3, out_sp...  90.5 us
    pallas_call x1, Pallas kernels, prep(): pl.pallas_call(prep_kernel, grid=(NZ,), in_specs=[table, table] + [wide]...  5.57 us
    ppermute x1, starting transfers between devices, body(): lax.ppermute(text, ('blk_2', 'uly_1'), [(0, 0), (1, 2), (2, 1), (3, 3)])  4.92 us
  transfers between devices with their start and end apart: 1, of which 0 were waited for; matrix products, arithmetic and copies ran while one was open for 1% of the time, Pallas kernels for 5%

profile of v2, /device:TPU:1, one launch (start us, length us, event | category | flops | bytes accessed | tf_op | source)
XLA Modules:
  0.0 110.8 jit_solution(7807173462137120776)
XLA Ops:
  0.6 0.8 stack.9
  1.4 0.8 stack.10
  2.2 4.9 %collective-permute-start = (bf16[5,2,16,128]{3,2,1,0:T(8,128)(2,1)S(1)}, bf16[5,2,16,128]{3,2,1,0:T(8,128)(2,1)S(1)}, u32[]{:S(2)}, u32[]{:S(2)}) collective-permute-start(bf16[5,2,16,128]{3,2,1,0:T(8,128)(2,1)S(1)} %maximum_bitcast_fusion), channel_id=1, source_target_pairs={{0,0},{1,8},{8,1},{9,9},{2,2},{3,10},{10,3},{11,11},{4,4},{5,12},{... | collective-permute-start | bytes 122888 | tf_op jit(solution)/shard_map/ppermute | solution.py:481
  7.9 0.8 sine_multiply_fusion
  8.7 0.1 compare_select_fusion
  8.7 5.6 %prep.1 = (bf16[40,40,128]{2,1,0:T(8,128)(2,1)}, bf16[40,40,128]{2,1,0:T(8,128)(2,1)}, bf16[40,40,128]{2,1,0:T(8,128)(2,1)}, bf16[40,40,128]{2,1,0:T(8,128)(2,1)}) custom-call(f32[40,128]{1,0:T(8,128)} %get-tuple-element.15.cos_ref, f32[40,128]{1,0:T(8,128)} %get-tuple-element.14.sin_ref, bf16[40,5120]{1,0:T(8,128)(2,1)} %q_ref.1, bf16[40,5120]{1,0:T(8,128)(2,1)} %k_ref.1, ...), custom_call_target="tpu_custom_call" | custom-call | tf_op jit(solution)/shard_map/prep/pallas_call | solution.py:62
  14.3 0.0 collective-permute-done.text
  14.3 0.0 copy-start.1
  14.3 1.5 %broadcast_in_dim.89.bias_a = f32[2560,128]{1,0:T(8,128)} broadcast(f32[2560]{0:T(1024)S(1)} %get-tuple-element.22), dimensions={0} | broadcast | bytes 1320960 | tf_op jit(solution)/shard_map/broadcast_in_dim | solution.py:496
  15.8 1.5 %broadcast_in_dim.90.bias_b = f32[2560,128]{1,0:T(8,128)} broadcast(f32[2560]{0:T(1024)S(1)} %get-tuple-element.23), dimensions={0} | broadcast | bytes 1320960 | tf_op jit(solution)/shard_map/broadcast_in_dim | solution.py:497
  17.3 0.0 copy-done.1
  17.3 90.5 %block.1 = (bf16[40,2,24,128]{3,2,1,0:T(8,128)(2,1)}, bf16[40,2,24,128]{3,2,1,0:T(8,128)(2,1)}, bf16[1280,128]{1,0:T(8,128)(2,1)}, bf16[1280,128]{1,0:T(8,128)(2...) custom-call(bf16[40,40,128]{2,1,0:T(8,128)(2,1)} %get-tuple-element., ...), custom_call_target="tpu_custom_call" | custom-call | tf_op jit(solution)/shard_map/block/pallas_call | solution.py:426
  107.8 0.0 copy-start
  107.8 1.2 %copy.18 = bf16[40,2,20,128]{3,0,2,1:T(8,128)(2,1)S(1)} copy(bf16[40,2,20,128]{3,2,1,0:T(8,128)(2,1)} %bitcast.26) | data formatting | bytes 819200 | tf_op jit(solution)/shard_map/slice | solution.py:502
  109.1 0.8 copy.27
  109.9 0.0 copy-done
  109.9 0.1 copy.20
  110.0 0.8 copy.26
  (8 shorter events, 0.1 us)
Async XLA Ops:
  2.2 12.1 %collective-permute-start = (bf16[5,2,16,128]{3,2,1,0:T(8,128)(2,1)S(1)}, bf16[5,2,16,128]{3,2,1,0:T(8,128)(2,1)S(1)}, u32[]{:S(2)}, u32[]{:S(2)}) collective-permute-start(bf16[5,2,16,128]{3,2,1,0:T(8,128)(2,1)S(1)} %maximum_bitcast_fusion), channel_id=1, source_target_pairs={{0,0},{1,8},{8,1},{9,9},{2,2},{3,10},{10,3},{11,11},{4,4},{5,12},{... | collective-permute-start | bytes 122888 | tf_op jit(solution)/shard_map/ppermute | solution.py:481
  14.3 3.0 %copy-start.1 = (bf16[5,2,16,128]{3,2,1,0:T(8,128)(2,1)}, bf16[5,2,16,128]{3,2,1,0:T(8,128)(2,1)S(1)}, u32[]{:S(2)}) copy-start(bf16[5,2,16,128]{3,2,1,0:T(8,128)(2,1)S(1)} %collective-permute-done.text) | copy-start | bytes 122884
  107.8 2.1 %copy-start = (bf16[40,2,24,128]{3,2,1,0:T(8,128)(2,1)S(1)}, bf16[40,2,24,128]{3,2,1,0:T(8,128)(2,1)}, u32[]{:S(2)}) copy-start(bf16[40,2,24,128]{3,2,1,0:T(8,128)(2,1)} %get-tuple-element.13) | copy-start | bytes 1474564
